TPU v7x, 256 devices: a whole 4x4x8 slice. The times are simulated.
256 devices in a mesh: member: 16 (over z, core), space: 16 (over x, y).
Axes of the slice: x: 4, y: 4, z: 8, core: 2. Of those that a mesh axis runs over, the one named last changes fastest.
Arguments:
- latents: bfloat16 [12288, 512], P('space'), may hold values from -6 to 6
- sample_perturbation: bfloat16 [48, 12288, 512], P('member', 'space'), may hold values from -6 to 6
- noise_table: float32 [64, 512], replicated, may hold values from 0.2 to 1.5
- member_seed: int32 [48], P('member'), may hold values from 0 to 63
- piece_arrangement: int32 [768], replicated, may hold values from 0 to 767, each once
- targets: bfloat16 [12288, 384], P('space'), may hold values from -4 to 4
- w_gate: bfloat16 [512, 1024], replicated, may hold values from -0.25 to 0.25
- w_up: bfloat16 [512, 1024], replicated, may hold values from -0.25 to 0.25
- lowering_matrix: bfloat16 [1024, 384], replicated, may hold values from -0.1875 to 0.1875
Outputs:
- latent_grad: float32 [12288, 512], P('space', 'member')
Inputs may be any that keep to these rules, and one draw needn't show every extreme that they name: `piece_arrangement`: a permutation of the 768 positions of a tile, the same for every tile.
All inputs are finite; a program needn't handle non-finite values.
Results may differ from a plain program's by a relative error of at most 0.0019.
Values may be sent and summed in bfloat16 or wider, within the bound.
No kernel may reach another device: no remote copies, remote signals or barrier semaphores. Data moves between devices by JAX's collectives and lax.ppermute only.
A program may use at most 128 MiB of HBM per device.

v0:
```python
import jax
import jax.numpy as jnp
from jax import lax
from jax.experimental import pallas as pl
from jax.experimental.pallas import tpu as pltpu
from jax.sharding import PartitionSpec as P

LAT = 512
HID = 1024
OUT = 384
PIECE = 8
GROUPS = 16
MINE = 48
LOCAL = 3
MEMBERS = 48
CHUNKS = (32, 16)
STARTS = (0, 32)
SCALE = float(PIECE * OUT) ** 0.5
F32 = jnp.float32
BF16 = jnp.bfloat16
VM = pl.BlockSpec(memory_space=pltpu.VMEM)
SM = pl.BlockSpec(memory_space=pltpu.SMEM)


def dot(a, b):
    return jnp.dot(a, b, preferred_element_type=F32)


def dot_t(a, b):
    return lax.dot_general(a, b, (((1,), (1,)), ((), ())), preferred_element_type=F32)


def pieces(x):
    high = x.astype(BF16)
    rest = x - high.astype(F32)
    mid = rest.astype(BF16)
    low = (rest - mid.astype(F32)).astype(BF16)
    return high, mid, low


def pack_kernel(me, seeds, order, latents, perturbation, table, targets, send0, send1, my_targets, pick):
    tokens = latents.shape[0]
    eye = lax.broadcasted_iota(jnp.int32, (128, 128), 0) == lax.broadcasted_iota(jnp.int32, (128, 128), 1)
    lane = lax.broadcasted_iota(jnp.int32, (128, tokens), 1)
    for b in range(tokens // 128):
        row = order[:, 128 * b : 128 * b + 128].astype(F32)
        column = jnp.sum(jnp.where(eye, row, 0.0), axis=1, keepdims=True).astype(jnp.int32)
        pick[128 * b : 128 * b + 128, :] = jnp.where(column == lane, 1.0, 0.0).astype(BF16)
    rows = latents[...].astype(F32)
    for m in range(LOCAL):
        factor = table[pl.ds(seeds[m], 1), :]
        noisy = (rows + perturbation[m].astype(F32) * factor).astype(BF16)
        moved = dot(pick[...], noisy).astype(BF16)
        for d in range(GROUPS):
            for send, start, count in zip((send0, send1), STARTS, CHUNKS):
                send[d, m * count : (m + 1) * count, :] = moved[d * MINE + start : d * MINE + start + count]
    mine = pick[pl.ds(pl.multiple_of(me[0] * MINE, 16), MINE), :]
    my_targets[...] = dot(mine, targets[...])


def score(forecast_ref, cotangent_ref, target, p, count):
    at = [pl.ds(p * PIECE + r, MEMBERS, stride=count) for r in range(PIECE)]
    u = jnp.concatenate([forecast_ref[j, a, :] for a in at for j in range(3)], axis=1)
    v = jnp.concatenate([target[p * PIECE + r : p * PIECE + r + 1, :] for r in range(PIECE)], axis=1)
    ub = u.astype(BF16)
    gram = dot_t(ub, ub)
    eye = lax.broadcasted_iota(jnp.int32, gram.shape, 0) == lax.broadcasted_iota(jnp.int32, gram.shape, 1)
    diagonal = jnp.where(eye, gram, 0.0)
    across = jnp.sum(diagonal, axis=1, keepdims=True)
    down = jnp.sum(diagonal, axis=0, keepdims=True)
    gap = across + down - 2.0 * gram
    weight = (1.0 / jnp.sqrt(jnp.where(eye, 0.0, gap) + 1.0)).astype(BF16)
    total = jnp.sum(weight.astype(F32), axis=1, keepdims=True)
    spread = (SCALE / MEMBERS * (total * u - dot(weight, ub))).astype(BF16)
    miss = u - v
    norm = jnp.sum(miss * miss, axis=1, keepdims=True)
    skill = miss * (1.0 / jnp.sqrt(norm + 1.0))
    cotangent = SCALE * skill - spread.astype(F32)
    for r, a in enumerate(at):
        for j in range(3):
            cotangent_ref[j, a, :] = cotangent[:, OUT * r + 128 * j : OUT * r + 128 * j + 128]


def network(noisy, target, w_gate, w_up, lowering, left, right, forecast, cotangent, count):
    total = MEMBERS * count
    block = 256

    @pl.loop(0, total // block)
    def _(i):
        at = pl.ds(pl.multiple_of(i * block, block), block)
        x = noisy[at, :]
        gate = dot(x, w_gate[...])
        up = dot(x, w_up[...])
        s = jax.nn.sigmoid(gate)
        swish = gate * s
        right[at, :] = swish
        left[at, :] = up * (s + swish * (1.0 - s))
        made = dot((swish * up).astype(BF16), lowering[...]).astype(BF16).astype(F32)
        for j in range(3):
            forecast[j, at, :] = made[:, 128 * j : 128 * j + 128]

    for p in range(count // PIECE):
        score(forecast, cotangent, target, p, count)

    token = lax.broadcasted_iota(jnp.int32, (count, block), 0)
    place = lax.broadcasted_iota(jnp.int32, (count, block), 1)
    gate_sum = jnp.zeros((count, HID), F32)
    up_sum = jnp.zeros((count, HID), F32)

    def step(i, carry):
        gate_sum, up_sum = carry
        at = pl.ds(pl.multiple_of(i * block, block), block)
        hidden_grad = dot_t(
            jnp.concatenate([cotangent[j, at, :] for j in range(3)], axis=1).astype(BF16), lowering[...]
        )
        gate_grad = (hidden_grad * left[at, :]).astype(BF16)
        up_grad = (hidden_grad * right[at, :]).astype(BF16)
        collect = jnp.where(lax.rem(place, count) == token, 1.0, 0.0).astype(BF16)
        return gate_sum + dot(collect, gate_grad), up_sum + dot(collect, up_grad)

    gate_sum, up_sum = lax.fori_loop(0, total // block, step, (gate_sum, up_sum))
    gates = dot_t(jnp.concatenate(pieces(gate_sum), axis=0), w_gate[...])
    ups = dot_t(jnp.concatenate(pieces(up_sum), axis=0), w_up[...])
    both = gates + ups
    return both[:count] + both[count : 2 * count] + both[2 * count :]


def first_kernel(noisy, target, w_gate, w_up, lowering, out, left, right, forecast, cotangent):
    grad = network(noisy, target[: CHUNKS[0]], w_gate, w_up, lowering, left, right, forecast, cotangent, CHUNKS[0])
    out[...] = grad


def last_kernel(noisy, target, w_gate, w_up, lowering, earlier, out, left, right, forecast, cotangent):
    grad = network(noisy, target[CHUNKS[0] :], w_gate, w_up, lowering, left, right, forecast, cotangent, CHUNKS[1])
    parts = (earlier[:16], earlier[16:], grad)
    blank = jnp.zeros((16, 32), F32)
    for d in range(GROUPS):
        out[d] = jnp.concatenate([part[:, 32 * d : 32 * d + 32] for part in parts] + [blank], axis=1)


def unpack_kernel(arrived, pick, out):
    flat = arrived[...].reshape(GROUPS * 16, 128)
    turned = flat.T
    total = jnp.zeros(out.shape, F32)
    for c in range(3):
        rows = jnp.concatenate([pick[d * MINE + 16 * c : d * MINE + 16 * c + 16, :] for d in range(GROUPS)], axis=0)
        placed = dot(jnp.concatenate(pieces(turned[32 * c : 32 * c + 32]), axis=0), rows)
        total = total + placed[:32] + placed[32:64] + placed[64:]
    out[...] = total


def call(kernel, out_shape, specs, scratch=(), flops=0):
    many = isinstance(out_shape, list)
    return pl.pallas_call(
        kernel,
        out_shape=out_shape,
        in_specs=specs,
        out_specs=[VM] * len(out_shape) if many else VM,
        scratch_shapes=list(scratch),
        compiler_params=pltpu.CompilerParams(vmem_limit_bytes=48 * 1024 * 1024),
        cost_estimate=pl.CostEstimate(flops=flops, transcendentals=0, bytes_accessed=0) if flops else None,
    )


def scratch(count):
    rows = MEMBERS * count
    return (
        pltpu.VMEM((rows, HID), F32),
        pltpu.VMEM((rows, HID), F32),
        pltpu.VMEM((3, rows, 128), F32),
        pltpu.VMEM((3, rows, 128), F32),
    )


def body(latents, perturbation, noise_table, member_seed, piece_arrangement, targets, w_gate, w_up, lowering_matrix):
    tokens = latents.shape[0]
    me = lax.axis_index("member").astype(jnp.int32).reshape(1)
    shape = jax.ShapeDtypeStruct
    sends = [shape((GROUPS, LOCAL * count, LAT), BF16) for count in CHUNKS]
    send0, send1, my_targets, pick = call(
        pack_kernel,
        [*sends, shape((MINE, OUT), F32), shape((tokens, tokens), BF16)],
        [SM, SM, VM, VM, VM, VM, VM],
    )(me, member_seed, piece_arrangement.reshape(1, tokens), latents, perturbation, noise_table, targets)
    got0 = lax.all_to_all(send0, "member", 0, 0, tiled=True)
    got1 = lax.all_to_all(send1, "member", 0, 0, tiled=True)
    earlier = call(first_kernel, shape((CHUNKS[0], LAT), F32), [VM] * 5, scratch(CHUNKS[0]), 10**10)(
        got0.reshape(MEMBERS * CHUNKS[0], LAT), my_targets, w_gate, w_up, lowering_matrix
    )
    packed = call(last_kernel, shape((GROUPS, 16, 128), F32), [VM] * 6, scratch(CHUNKS[1]), 5 * 10**9)(
        got1.reshape(MEMBERS * CHUNKS[1], LAT), my_targets, w_gate, w_up, lowering_matrix, earlier
    )
    arrived = lax.all_to_all(packed, "member", 0, 0, tiled=True)
    columns = call(unpack_kernel, shape((LAT // GROUPS, tokens), F32), [VM] * 2)(arrived, pick)
    return columns.T


def solution(mesh):
    in_specs = (
        P("space", None),
        P("member", "space", None),
        P(),
        P("member"),
        P(),
        P("space", None),
        P(),
        P(),
        P(),
    )
    return jax.shard_map(body, mesh=mesh, in_specs=in_specs, out_specs=P("space", "member"), check_vma=False)
```

profile of v0, /device:TPU:1, one launch (start us, length us, event | category | flops | bytes accessed | tf_op | source)
XLA Modules:
  0.0 113.9 jit_solution(989583916841871839)
XLA Ops:
  0.0 0.7 reshape.13.order
  0.7 0.0 copy-start
  0.7 1.1 copy-done
  1.8 0.0 copy-start.1
  1.8 1.1 copy-done.1
  2.9 0.0 copy-start.2
  2.9 0.9 copy-done.2
  3.8 0.0 copy-start.3
  3.8 0.7 copy-done.3
  4.4 4.8 %shard_map.91 = (bf16[16,96,512]{2,1,0:T(8,128)(2,1)S(1)}, bf16[16,48,512]{2,1,0:T(8,128)(2,1)}, f32[48,384]{1,0:T(8,128)S(1)}, bf16[768,768]{1,0:T(8,128)(2,1)S(1)}) custom-call(s32[1]{0:T(128)} %bitcast.me, s32[3]{0:T(128)S(1)} %copy-done.3, s32[1,768]{1,0:T(1,128)S(1)} %reshape.13.order, bf16[768,512]{1,0:T(8,128)(2,1)S(1)} %copy-done, ...), custom_call_target="tpu_custom_call" | custom-call | tf_op jit(solution)/shard_map/pallas_call | solution.py:180
  9.3 49.4 %all_to_all.15 = bf16[16,96,512]{2,1,0:T(8,128)(2,1)S(1)} all-to-all(bf16[16,96,512]{2,1,0:T(8,128)(2,1)S(1)} %get-tuple-element.11), channel_id=1, replica_groups=mesh['member'=16,'space'=16] {'member'}, dimensions={0} | all-to-all | bytes 3145728 | tf_op jit(solution)/shard_map/all_to_all | solution.py:185
  58.7 0.0 copy-done.10
  58.7 3.7 %all-to-all-start = ((bf16[16,48,512]{2,1,0:T(8,128)(2,1)}), bf16[16,48,512]{2,1,0:T(8,128)(2,1)S(1)}, u32[]{:S(2)}, u32[]{:S(2)}) async-start(bf16[16,48,512]{2,1,0:T(8,128)(2,1)} %get-tuple-element.9), calls=%async_computation | async-start | bytes 1572864 | tf_op jit(solution)/shard_map/all_to_all | solution.py:186
  62.4 0.0 copy-start.4
  62.4 1.2 %copy-done.4 = bf16[512,1024]{1,0:T(8,128)(2,1)S(1)} copy-done((bf16[512,1024]{1,0:T(8,128)(2,1)S(1)}, bf16[512,1024]{1,0:T(8,128)(2,1)}, u32[]{:S(2)}) %copy-start.4) | copy-done | bytes 1048600
  63.6 0.0 copy-start.6
  63.6 1.2 %copy-done.6 = bf16[512,1024]{1,0:T(8,128)(2,1)S(1)} copy-done((bf16[512,1024]{1,0:T(8,128)(2,1)S(1)}, bf16[512,1024]{1,0:T(8,128)(2,1)}, u32[]{:S(2)}) %copy-start.6) | copy-done | bytes 1048600
  64.8 0.0 copy-start.8
  64.8 1.1 copy-done.8
  66.0 0.0 copy-start.11
  66.0 0.9 copy-done.11
  66.9 16.9 %shard_map.92.earlier = f32[32,512]{1,0:T(8,128)S(1)} custom-call(bf16[1536,512]{1,0:T(8,128)(2,1)S(1)} %bitcast.4, f32[48,384]{1,0:T(8,128)S(1)} %copy-done.11, bf16[512,1024]{1,0:T(8,128)(2,1)S(1)} %copy-done.4, bf16[512,1024]{1,0:T(8,128)(2,1)S(1)} %copy-done.6, bf16[1024,384]{1,0:T(8,128)(2,1)S(1)} %copy-done.8), custom_call_target="tpu_custom_call" | custom-call | flops 10000000000 | tf_op jit(solution)/shard_map/pallas_call | solution.py:187
  83.8 0.7 copy-done.13
  84.4 0.0 all-to-all-done
  84.4 1.2 %copy-done.5 = bf16[512,1024]{1,0:T(8,128)(2,1)S(1)} copy-done((bf16[512,1024]{1,0:T(8,128)(2,1)S(1)}, bf16[512,1024]{1,0:T(8,128)(2,1)}, u32[]{:S(2)}) %copy-start.5) | copy-done | bytes 1048600
  85.7 1.2 %copy-done.7 = bf16[512,1024]{1,0:T(8,128)(2,1)S(1)} copy-done((bf16[512,1024]{1,0:T(8,128)(2,1)S(1)}, bf16[512,1024]{1,0:T(8,128)(2,1)}, u32[]{:S(2)}) %copy-start.7) | copy-done | bytes 1048600
  86.9 1.1 copy-done.9
  88.0 0.9 copy-done.12
  88.9 0.8 copy-done.14
  89.8 7.9 %shard_map.93 = f32[16,16,128]{2,1,0:T(8,128)S(1)} custom-call(bf16[768,512]{1,0:T(8,128)(2,1)S(1)} %bitcast.5, f32[48,384]{1,0:T(8,128)S(1)} %copy-done.12, bf16[512,1024]{1,0:T(8,128)(2,1)S(1)} %copy-done.5, bf16[512,1024]{1,0:T(8,128)(2,1)S(1)} %copy-done.7, bf16[1024,384]{1,0:T(8,128)(2,1)S(1)} %copy-done.9, f32[32,512]{1,0:T(8,128)S(1)} %copy-done.14), custom_call_target="tpu_custom_call" | custom-call | flops 5000000000 | tf_op jit(solution)/shard_map/pallas_call | solution.py:190
  97.7 15.2 %all_to_all.16.arrived = f32[16,16,128]{2,1,0:T(8,128)S(1)} all-to-all(f32[16,16,128]{2,1,0:T(8,128)S(1)} %shard_map.93), channel_id=1, replica_groups=mesh['member'=16,'space'=16] {'member'}, dimensions={0} | all-to-all | bytes 262144 | tf_op jit(solution)/shard_map/all_to_all | solution.py:193
  112.9 1.0 shard_map.94
  (7 shorter events, 0.0 us)
Async XLA Ops:
  0.7 1.1 copy-start
  1.8 1.1 copy-start.1
  2.9 0.9 copy-start.2
  3.8 0.7 copy-start.3
  9.3 49.4 %copy-start.10 = (f32[48,384]{1,0:T(8,128)}, f32[48,384]{1,0:T(8,128)S(1)}, u32[]{:S(2)}) copy-start(f32[48,384]{1,0:T(8,128)S(1)} %get-tuple-element.10.target) | copy-start | bytes 221188
  58.7 25.7 %all-to-all-start = ((bf16[16,48,512]{2,1,0:T(8,128)(2,1)}), bf16[16,48,512]{2,1,0:T(8,128)(2,1)S(1)}, u32[]{:S(2)}, u32[]{:S(2)}) async-start(bf16[16,48,512]{2,1,0:T(8,128)(2,1)} %get-tuple-element.9), calls=%async_computation | async-start | bytes 1572864 | tf_op jit(solution)/shard_map/all_to_all | solution.py:186
  62.4 1.2 %copy-start.4 = (bf16[512,1024]{1,0:T(8,128)(2,1)S(1)}, bf16[512,1024]{1,0:T(8,128)(2,1)}, u32[]{:S(2)}) copy-start(bf16[512,1024]{1,0:T(8,128)(2,1)} %w_gate.3) | copy-start | bytes 3145732
  63.6 1.2 %copy-start.6 = (bf16[512,1024]{1,0:T(8,128)(2,1)S(1)}, bf16[512,1024]{1,0:T(8,128)(2,1)}, u32[]{:S(2)}) copy-start(bf16[512,1024]{1,0:T(8,128)(2,1)} %w_up.3) | copy-start | bytes 3145732
  64.8 1.1 copy-start.8
  66.0 0.9 copy-start.11
  83.8 0.7 copy-start.13
  84.4 1.2 %copy-start.5 = (bf16[512,1024]{1,0:T(8,128)(2,1)S(1)}, bf16[512,1024]{1,0:T(8,128)(2,1)}, u32[]{:S(2)}) copy-start(bf16[512,1024]{1,0:T(8,128)(2,1)} %w_gate.3) | copy-start | bytes 3145732
  85.7 1.2 %copy-start.7 = (bf16[512,1024]{1,0:T(8,128)(2,1)S(1)}, bf16[512,1024]{1,0:T(8,128)(2,1)}, u32[]{:S(2)}) copy-start(bf16[512,1024]{1,0:T(8,128)(2,1)} %w_up.3) | copy-start | bytes 3145732
  86.9 1.1 copy-start.9
  88.0 0.9 copy-start.12
  88.9 0.8 copy-start.14
where the time goes:
time: 115 us; the launch traced here: 114 us
  blocking collectives  64.6 us (56%)
  Pallas kernels  30.7 us (27%)
  local copies, waits for them, and re-layouts  14.9 us (13%)
  starting transfers between devices  3.69 us (3%)
    all_to_all x1, blocking collectives, body(): got0 = lax.all_to_all(send0, 'member', 0, 0, tiled=True)  49.4 us
    pallas_call x1, Pallas kernels, body(): call(first_kernel, shape((CHUNKS[0], LAT), F32), [VM] * 5, scratch(CHUNKS...  16.9 us
    all_to_all x1, blocking collectives, body(): arrived = lax.all_to_all(packed, 'member', 0, 0, tiled=True)  15.2 us
    unnamed x30, local copies, waits for them, and re-layouts  14.2 us
    pallas_call x1, Pallas kernels, body(): call(last_kernel, shape((GROUPS, 16, 128), F32), [VM] * 6, scratch(CHUNKS...  7.92 us
    pallas_call x1, Pallas kernels, body(): call(pack_kernel, [*sends, shape((MINE, OUT), F32), shape((tokens, tokens...  4.81 us
    all_to_all x1, starting transfers between devices, body(): got1 = lax.all_to_all(send1, 'member', 0, 0, tiled=True)  3.69 us
  transfers between devices with their start and end apart: 1, of which 0 were waited for; matrix products, arithmetic and copies ran while one was open for 0% of the time, Pallas kernels for 15%

commit v1 on v0

v1 whole, which is shorter than its diff:
```python
import jax
import jax.numpy as jnp
from jax import lax
from jax.experimental import pallas as pl
from jax.experimental.pallas import tpu as pltpu
from jax.sharding import PartitionSpec as P


LAT = 512
HID = 1024
OUT = 384
PIECE = 8
BLOCK = 256
PAD = 8
GROUPS = 16
MINE = 48
LOCAL = 3
MEMBERS = 48
Z = 8
OFFSETS = tuple((dz, dc) for dz in (0, 3, 5, 4, 2, 6, 1, 7) for dc in (0, 1))
CHUNKS = (32, 16)
STARTS = (0, 32)
SCALE = float(PIECE * OUT) ** 0.5
F32 = jnp.float32
BF16 = jnp.bfloat16
VM = pl.BlockSpec(memory_space=pltpu.VMEM)
SM = pl.BlockSpec(memory_space=pltpu.SMEM)
HB = pl.BlockSpec(memory_space=pltpu.HBM)


def far(x):
    return pltpu.with_memory_space_constraint(x, pltpu.HBM)


def dot(a, b):
    return jnp.dot(a, b, preferred_element_type=F32)


def dot_t(a, b):
    return lax.dot_general(a, b, (((1,), (1,)), ((), ())), preferred_element_type=F32)


def pieces(x):
    high = x.astype(BF16)
    rest = x - high.astype(F32)
    mid = rest.astype(BF16)
    low = (rest - mid.astype(F32)).astype(BF16)
    return high, mid, low


def columns_of(order):
    eye = lax.broadcasted_iota(jnp.int32, (128, 128), 0) == lax.broadcasted_iota(jnp.int32, (128, 128), 1)
    found = []
    for b in range(order.shape[1] // 128):
        row = order[:, 128 * b : 128 * b + 128].astype(F32)
        found.append(jnp.sum(jnp.where(eye, row, 0.0), axis=1, keepdims=True).astype(jnp.int32))
    return found


def one_hot(columns, start, count, tokens):
    lane = lax.broadcasted_iota(jnp.int32, (16, tokens), 1)
    parts = []
    for d in range(GROUPS):
        for first in range(d * MINE + start, d * MINE + start + count, 16):
            column = columns[first // 128][first % 128 : first % 128 + 16]
            parts.append(jnp.where(column == lane, 1.0, 0.0).astype(BF16))
    return jnp.concatenate(parts, axis=0)


def move(noisy, picked, send, count):
    for m in range(LOCAL):
        moved = dot(picked, noisy(m)).astype(BF16)
        for d in range(GROUPS):
            send[d, m * count : (m + 1) * count, :] = moved[d * count : (d + 1) * count]


def load_state(seeds, latents, perturbation, table, seeds_here, latents_here, here, table_here, sems):
    copies = [
        pltpu.make_async_copy(seeds, seeds_here, sems.at[0]),
        pltpu.make_async_copy(table, table_here, sems.at[1]),
        pltpu.make_async_copy(latents, latents_here, sems.at[2]),
    ] + [pltpu.make_async_copy(perturbation.at[m], here.at[m], sems.at[3 + m]) for m in range(LOCAL)]
    for copy in copies:
        copy.start()

    def noisy(m):
        if m == 0:
            for copy in copies[:3]:
                copy.wait()
        copies[3 + m].wait()
        factor = table_here[pl.ds(seeds_here[m], 1), :]
        return (latents_here[...].astype(F32) + here[m].astype(F32) * factor).astype(BF16)

    return noisy


def early_kernel(order, seeds, latents, perturbation, table, send, *state):
    noisy = load_state(seeds, latents, perturbation, table, *state)
    picked = one_hot(columns_of(order[...]), STARTS[0], CHUNKS[0], latents.shape[0])
    move(noisy, picked, send, CHUNKS[0])


def late_kernel(me, order, seeds, latents, perturbation, table, *rest):
    sends, pick, state = rest[:GROUPS], rest[GROUPS], rest[GROUPS + 1 :]
    noisy = load_state(seeds, latents, perturbation, table, *state)
    pick[...] = one_hot(columns_of(order[...]), 0, MINE, latents.shape[0])
    z, core = me[0] // 2, lax.rem(me[0], 2)
    count = CHUNKS[1]
    parts = []
    for dz, dc in OFFSETS:
        there = lax.rem(z + dz, Z) * 2 + (1 - core if dc else core)
        parts.append(pick[pl.ds(pl.multiple_of(there * MINE + STARTS[1], 16), count), :])
    picked = jnp.concatenate(parts, axis=0)
    for m in range(LOCAL):
        moved = dot(picked, noisy(m)).astype(BF16)
        for k, send in enumerate(sends):
            send[m * count : (m + 1) * count, :] = moved[k * count : (k + 1) * count]


def target_kernel(me, pick, targets, my_targets):
    my_targets[...] = dot(pick[pl.ds(pl.multiple_of(me[0] * MINE, 16), MINE), :], targets[...])


def score(forecast, cotangent, target, p, gap_rows):
    def token(r):
        at = pl.ds(p * PIECE + r, MEMBERS, stride=gap_rows)
        u = jnp.concatenate([forecast[j, at, :] for j in range(3)], axis=1)
        return at, u, u - target[p * PIECE + r : p * PIECE + r + 1, :]

    gram = jnp.zeros((MEMBERS, MEMBERS), F32)
    norm = jnp.zeros((MEMBERS, 128), F32)
    for r in range(PIECE):
        at, u, miss = token(r)
        ub = u.astype(BF16)
        gram = gram + dot_t(ub, ub)
        square = miss * miss
        norm = norm + square[:, :128] + square[:, 128:256] + square[:, 256:]
    eye = lax.broadcasted_iota(jnp.int32, gram.shape, 0) == lax.broadcasted_iota(jnp.int32, gram.shape, 1)
    diagonal = jnp.where(eye, gram, 0.0)
    across = jnp.sum(diagonal, axis=1, keepdims=True)
    down = jnp.sum(diagonal, axis=0, keepdims=True)
    gap = across + down - 2.0 * gram
    weight = (1.0 / jnp.sqrt(jnp.where(eye, 0.0, gap) + 1.0)).astype(BF16)
    total = jnp.sum(weight.astype(F32), axis=1, keepdims=True)
    skill = SCALE / jnp.sqrt(jnp.sum(norm, axis=1, keepdims=True) + 1.0)
    for r in range(PIECE):
        at, u, miss = token(r)
        spread = (SCALE / MEMBERS * (total * u - dot(weight, u.astype(BF16)))).astype(BF16)
        made = skill * miss - spread.astype(F32)
        for j in range(3):
            cotangent[j, at, :] = made[:, 128 * j : 128 * j + 128]


def network(noisy, target, w_gate, w_up, lowering, state, count, start):
    left, right, forecast, cotangent, gate_sum, up_sum, target_here, sem = state[:8]
    copy = pltpu.make_async_copy(target.at[pl.ds(start, count)], target_here, sem)
    copy.start()
    total = MEMBERS * count
    block = BLOCK
    inside = block // count
    gap_rows = count + PAD

    @pl.loop(0, total // block)
    def _(i):
        at = pl.ds(pl.multiple_of(i * block, block), block)
        x = noisy[at, :]
        half = 0.5 * dot(x, w_gate[...])
        up = dot(x, w_up[...])
        bent = 1.0 + jnp.tanh(half)
        swish = half * bent
        s = 0.5 * bent
        right[at, :] = swish
        left[at, :] = up * (s + swish * (1.0 - s))
        made = dot((swish * up).astype(BF16), lowering[...]).astype(BF16).astype(F32)
        for q in range(inside):
            to = pl.ds(pl.multiple_of(i * inside * gap_rows + q * gap_rows, 8), count)
            for j in range(3):
                forecast[j, to, :] = made[count * q : count * q + count, 128 * j : 128 * j + 128]

    copy.wait()
    for p in range(count // PIECE):
        score(forecast, cotangent, target_here, p, gap_rows)

    token = lax.broadcasted_iota(jnp.int32, (count, block), 0)
    place = lax.broadcasted_iota(jnp.int32, (count, block), 1)
    collect = jnp.where(lax.rem(place, count) == token, 1.0, 0.0).astype(BF16)
    gate_sum[...] = jnp.zeros((count, HID), F32)
    up_sum[...] = jnp.zeros((count, HID), F32)

    @pl.loop(0, total // block)
    def _(i):
        at = pl.ds(pl.multiple_of(i * block, block), block)
        rows = []
        for q in range(inside):
            back = pl.ds(pl.multiple_of(i * inside * gap_rows + q * gap_rows, 8), count)
            rows.append(jnp.concatenate([cotangent[j, back, :] for j in range(3)], axis=1))
        hidden_grad = dot_t(jnp.concatenate(rows, axis=0).astype(BF16), lowering[...])
        gate_sum[...] += dot(collect, (hidden_grad * left[at, :]).astype(BF16))
        up_sum[...] += dot(collect, (hidden_grad * right[at, :]).astype(BF16))

    gates = dot_t(jnp.concatenate(pieces(gate_sum[...]), axis=0), w_gate[...])
    ups = dot_t(jnp.concatenate(pieces(up_sum[...]), axis=0), w_up[...])
    both = gates + ups
    return both[:count] + both[count : 2 * count] + both[2 * count :]


def first_kernel(noisy, target, w_gate, w_up, lowering, out, gate_here, up_here, low_here, *state):
    here, sem, sems = state[-3:]
    copies = [
        pltpu.make_async_copy(w_gate, gate_here, sems.at[0]),
        pltpu.make_async_copy(w_up, up_here, sems.at[1]),
        pltpu.make_async_copy(lowering, low_here, sems.at[2]),
    ]
    for copy in copies:
        copy.start()
    for copy in copies:
        copy.wait()
    here[...] = network(noisy, target, gate_here, up_here, low_here, state, CHUNKS[0], STARTS[0])
    copy = pltpu.make_async_copy(here, out, sem)
    copy.start()
    copy.wait()


def last_kernel(*refs):
    gathered, (target, w_gate, w_up, lowering, earlier, out), state = refs[:GROUPS], refs[GROUPS : GROUPS + 6], refs[GROUPS + 6 :]
    here, sem, noisy = state[-3:]
    copy = pltpu.make_async_copy(earlier, here, sem)
    copy.start()
    size = LOCAL * CHUNKS[1]
    for k, part in enumerate(gathered):
        noisy[k * size : (k + 1) * size, :] = part[...]
    grad = network(noisy, target, w_gate, w_up, lowering, state, CHUNKS[1], STARTS[1])
    copy.wait()
    parts = (here[:16], here[16:], grad)
    blank = jnp.zeros((16, 32), F32)
    for d in range(GROUPS):
        out[d] = jnp.concatenate([part[:, 32 * d : 32 * d + 32] for part in parts] + [blank], axis=1)


def unpack_kernel(arrived, pick, out):
    flat = arrived[...].reshape(GROUPS * 16, 128)
    turned = flat.T
    total = jnp.zeros(out.shape, F32)
    for c in range(3):
        rows = jnp.concatenate([pick[d * MINE + 16 * c : d * MINE + 16 * c + 16, :] for d in range(GROUPS)], axis=0)
        placed = dot(jnp.concatenate(pieces(turned[32 * c : 32 * c + 32]), axis=0), rows)
        total = total + placed[:32] + placed[32:64] + placed[64:]
    out[...] = total


def call(kernel, out_shape, specs, out_specs, scratch=(), flops=0, megabytes=24):
    return pl.pallas_call(
        kernel,
        out_shape=out_shape,
        in_specs=specs,
        out_specs=out_specs,
        scratch_shapes=list(scratch),
        compiler_params=pltpu.CompilerParams(vmem_limit_bytes=megabytes * 1024 * 1024),
        cost_estimate=pl.CostEstimate(flops=flops, transcendentals=0, bytes_accessed=0) if flops else None,
    )


def scratch(count):
    rows = MEMBERS * count
    padded = MEMBERS * (count + PAD)
    return (
        pltpu.VMEM((rows, HID), F32),
        pltpu.VMEM((rows, HID), F32),
        pltpu.VMEM((3, padded, 128), F32),
        pltpu.VMEM((3, padded, 128), F32),
        pltpu.VMEM((count, HID), F32),
        pltpu.VMEM((count, HID), F32),
        pltpu.VMEM((count, OUT), F32),
        pltpu.SemaphoreType.DMA,
        pltpu.VMEM((CHUNKS[0], LAT), F32),
        pltpu.SemaphoreType.DMA,
    )


def body(latents, perturbation, noise_table, member_seed, piece_arrangement, targets, w_gate, w_up, lowering_matrix):
    tokens = latents.shape[0]
    latents, perturbation, noise_table, member_seed, targets = (
        far(x) for x in (latents, perturbation, noise_table, member_seed, targets)
    )
    me = lax.axis_index("member").astype(jnp.int32).reshape(1)
    shape = jax.ShapeDtypeStruct
    order = piece_arrangement.reshape(1, tokens)
    state = (
        pltpu.SMEM((LOCAL,), jnp.int32),
        pltpu.VMEM((tokens, LAT), BF16),
        pltpu.VMEM((LOCAL, tokens, LAT), BF16),
        pltpu.VMEM(noise_table.shape, F32),
        pltpu.SemaphoreType.DMA((3 + LOCAL,)),
    )
    send0 = call(early_kernel, shape((GROUPS, LOCAL * CHUNKS[0], LAT), BF16), [VM] + [HB] * 4, VM, state, megabytes=20)(
        order, member_seed, latents, perturbation, noise_table
    )
    got0 = lax.all_to_all(send0, "member", 0, 0, tiled=True)
    *sends, pick = call(
        late_kernel,
        [shape((LOCAL * CHUNKS[1], LAT), BF16)] * GROUPS + [shape((tokens, tokens), BF16)],
        [SM, VM] + [HB] * 4,
        [VM] * (GROUPS + 1),
        state,
        flops=10**9,
        megabytes=20,
    )(me, order, member_seed, latents, perturbation, noise_table)
    got1 = []
    for (dz, dc), send in zip(OFFSETS, sends):
        pairs = [(2 * z + c, (z + dz) % Z * 2 + (c ^ dc)) for z in range(Z) for c in range(2)]
        got1.append(send if dz == dc == 0 else lax.ppermute(send, "member", pairs))
    my_targets = call(target_kernel, pltpu.HBM((MINE, OUT), F32), [SM, VM, VM], VM, flops=10**7, megabytes=4)(
        me, pick, targets
    )
    my_targets = far(my_targets)
    weights = tuple(far(w) for w in (w_gate, w_up, lowering_matrix))
    earlier, *weights = call(
        first_kernel,
        [pltpu.HBM((CHUNKS[0], LAT), F32), *(shape(w.shape, BF16) for w in weights)],
        [VM] + [HB] * 4,
        [HB] + [VM] * 3,
        (*scratch(CHUNKS[0]), pltpu.SemaphoreType.DMA((3,))),
        10**10,
        32,
    )(got0.reshape(MEMBERS * CHUNKS[0], LAT), my_targets, *weights)
    extra = (*scratch(CHUNKS[1]), pltpu.VMEM((MEMBERS * CHUNKS[1], LAT), BF16))
    packed = call(
        last_kernel, shape((GROUPS, 16, 128), F32), [VM] * GROUPS + [HB, VM, VM, VM, HB], VM, extra, 5 * 10**9, 24
    )(*got1, my_targets, *weights, far(earlier))
    arrived = lax.all_to_all(packed, "member", 0, 0, tiled=True)
    columns = call(unpack_kernel, shape((LAT // GROUPS, tokens), F32), [VM] * 2, VM)(arrived, pick)
    return columns.T


def solution(mesh):
    in_specs = (
        P("space", None),
        P("member", "space", None),
        P(),
        P("member"),
        P(),
        P("space", None),
        P(),
        P(),
        P(),
    )
    return jax.shard_map(body, mesh=mesh, in_specs=in_specs, out_specs=P("space", "member"), check_vma=False)
```

time: 115 us -> 115 us (level)
  blocking collectives: 64.6 us -> 12.9 us
  starting transfers between devices: 3.69 us -> 43.4 us
  waiting for transfers between devices: 0.01 us -> 21.7 us
  local copies, waits for them, and re-layouts: 14.9 us -> 1.3 us
  Pallas kernels: 30.7 us -> 35.6 us
    all_to_all x1 -> x0, blocking collectives: 49.4 us -> none  [body(): got0 = lax.all_to_all(send0, 'member', 0, 0, tiled=True)]
    ppermute x0 -> x15, starting transfers between devices: none -> 33.4 us  [body(): got1.append(send if dz == dc == 0 else lax.ppermute(send, 'member', pairs))]
    ppermute x0 -> x15, waiting for transfers between devices: none -> 21.7 us  [body(): got1.append(send if dz == dc == 0 else lax.ppermute(send, 'member', pairs))]
    unnamed x30 -> x4, local copies, waits for them, and re-layouts: 14.2 us -> 0.61 us
    all_to_all x1, starting transfers between devices: 3.69 us -> 9.98 us  [body(): got0 = lax.all_to_all(send0, 'member', 0, 0, tiled=True)]
    pallas_call x4 -> x6, Pallas kernels: 30.7 us -> 35.6 us  [the longest x1 16.5 us: body(): call(first_kernel, [pltpu.HBM((CHUNKS[0], LAT), F32), *(shape(w.shape, BF...]
    all_to_all x1, blocking collectives: 15.2 us -> 12.9 us  [body(): arrived = lax.all_to_all(packed, 'member', 0, 0, tiled=True)]
  transfers between devices with their start and end apart: 1 -> 16, of which waited for: 0 -> 2; matrix products, arithmetic and copies ran while one was open for 0% -> 0% of each run, Pallas kernels for 15% -> 18%
where the time goes in v1:
time: 115 us
  starting transfers between devices  43.4 us (38%)
  Pallas kernels  35.6 us (31%)
  waiting for transfers between devices  21.7 us (19%)
  blocking collectives  12.9 us (11%)
  local copies, waits for them, and re-layouts  1.3 us (1%)
    ppermute x15, starting transfers between devices, body(): got1.append(send if dz == dc == 0 else lax.ppermute(send, 'member', pairs))  33.4 us
    ppermute x15, waiting for transfers between devices, body(): got1.append(send if dz == dc == 0 else lax.ppermute(send, 'member', pairs))  21.7 us
    pallas_call x1, Pallas kernels, body(): call(first_kernel, [pltpu.HBM((CHUNKS[0], LAT), F32), *(shape(w.shape, BF...  16.5 us
    all_to_all x1, blocking collectives, body(): arrived = lax.all_to_all(packed, 'member', 0, 0, tiled=True)  12.9 us
    all_to_all x1, starting transfers between devices, body(): got0 = lax.all_to_all(send0, 'member', 0, 0, tiled=True)  9.98 us
    pallas_call x1, Pallas kernels, body(): call(last_kernel, shape((GROUPS, 16, 128), F32), [VM] * GROUPS + [HB, VM,...  8.74 us
    pallas_call x1, Pallas kernels, body(): call(early_kernel, shape((GROUPS, LOCAL * CHUNKS[0], LAT), BF16), [VM] +...  4.6 us
    pallas_call x1, Pallas kernels, body(): call(late_kernel, [shape((LOCAL * CHUNKS[1], LAT), BF16)] * GROUPS + [sha...  2.83 us
  transfers between devices with their start and end apart: 16, of which 2 were waited for; matrix products, arithmetic and copies ran while one was open for 0% of the time, Pallas kernels for 18%

profile of v1, /device:TPU:1, one launch (start us, length us, event | category | flops | bytes accessed | tf_op | source)
XLA Modules:
  0.0 115.0 jit_solution(984765764091861233)
XLA Ops:
  0.0 0.7 reshape.10.order
  0.7 4.6 %shard_map.93 = bf16[16,96,512]{2,1,0:T(8,128)(2,1)} custom-call(s32[1,768]{1,0:T(1,128)S(1)} %reshape.10.order, s32[3]{0:T(128)} %seeds.3, bf16[768,512]{1,0:T(8,128)(2,1)} %latents.3, bf16[3,768,512]{2,1,0:T(8,128)(2,1)} %perturbation.3, f32[64,512]{1,0:T(8,128)} %table.3), custom_call_target="tpu_custom_call" | custom-call | tf_op jit(solution)/shard_map/pallas_call | solution.py:295
  5.3 10.0 %all-to-all-start = ((bf16[16,96,512]{2,1,0:T(8,128)(2,1)}), bf16[16,96,512]{2,1,0:T(8,128)(2,1)S(1)}, u32[]{:S(2)}, u32[]{:S(2)}) async-start(bf16[16,96,512]{2,1,0:T(8,128)(2,1)} %shard_map.93), calls=%async_computation | async-start | bytes 3145728 | tf_op jit(solution)/shard_map/all_to_all | solution.py:298
  15.3 2.8 %shard_map.91 = (bf16[48,512]{1,0:T(8,128)(2,1)S(1)}, bf16[48,512]{1,0:T(8,128)(2,1)S(1)}, bf16[48,512]{1,0:T(8,128)(2,1)S(1)}, bf16[48,512]{1,0:T(8,128)(2,1)S(...) custom-call(s32[1]{0:T(128)} %bitcast.me, ...), custom_call_target="tpu_custom_call" | custom-call | flops 1000000000 | tf_op jit(solution)/shard_map/pallas_call | solution.py:299
  18.1 0.6 copy-done
  18.7 0.1 collective-permute-start
  18.8 3.4 %collective-permute-start.1 = (bf16[48,512]{1,0:T(8,128)(2,1)S(1)}, bf16[48,512]{1,0:T(8,128)(2,1)S(1)}, u32[]{:S(2)}, u32[]{:S(2)}) collective-permute-start(bf16[48,512]{1,0:T(8,128)(2,1)S(1)} %get-tuple-element.28), channel_id=1, source_target_pairs={{0,96},{16,112},{32,128},{48,144},{64,160},{80,176},{96,192},{112,... | collective-permute-start | bytes 147464 | tf_op jit(solution)/shard_map/ppermute | solution.py:311
  22.3 2.7 %collective-permute-start.2 = (bf16[48,512]{1,0:T(8,128)(2,1)S(1)}, bf16[48,512]{1,0:T(8,128)(2,1)S(1)}, u32[]{:S(2)}, u32[]{:S(2)}) collective-permute-start(bf16[48,512]{1,0:T(8,128)(2,1)S(1)} %get-tuple-element.29), channel_id=1, source_target_pairs={{0,112},{16,96},{32,144},{48,128},{64,176},{80,160},{96,208},{112,... | collective-permute-start | bytes 147464 | tf_op jit(solution)/shard_map/ppermute | solution.py:311
  25.0 2.1 %collective-permute-start.3 = (bf16[48,512]{1,0:T(8,128)(2,1)S(1)}, bf16[48,512]{1,0:T(8,128)(2,1)S(1)}, u32[]{:S(2)}, u32[]{:S(2)}) collective-permute-start(bf16[48,512]{1,0:T(8,128)(2,1)S(1)} %get-tuple-element.30), channel_id=1, source_target_pairs={{0,160},{16,176},{32,192},{48,208},{64,224},{80,240},{96,0},{112,1... | collective-permute-start | bytes 147464 | tf_op jit(solution)/shard_map/ppermute | solution.py:311
  27.0 1.5 %collective-permute-start.4 = (bf16[48,512]{1,0:T(8,128)(2,1)S(1)}, bf16[48,512]{1,0:T(8,128)(2,1)S(1)}, u32[]{:S(2)}, u32[]{:S(2)}) collective-permute-start(bf16[48,512]{1,0:T(8,128)(2,1)S(1)} %get-tuple-element.31), channel_id=1, source_target_pairs={{0,176},{16,160},{32,208},{48,192},{64,240},{80,224},{96,16},{112,... | collective-permute-start | bytes 147464 | tf_op jit(solution)/shard_map/ppermute | solution.py:311
  28.5 0.0 collective-permute-done.refs_1_
  28.5 5.4 %collective-permute-start.5 = (bf16[48,512]{1,0:T(8,128)(2,1)S(1)}, bf16[48,512]{1,0:T(8,128)(2,1)S(1)}, u32[]{:S(2)}, u32[]{:S(2)}) collective-permute-start(bf16[48,512]{1,0:T(8,128)(2,1)S(1)} %get-tuple-element.32), channel_id=1, source_target_pairs={{0,128},{16,144},{32,160},{48,176},{64,192},{80,208},{96,224},{112... | collective-permute-start | bytes 147464 | tf_op jit(solution)/shard_map/ppermute | solution.py:311
  33.9 21.2 %collective-permute-done.1.refs_2_ = bf16[48,512]{1,0:T(8,128)(2,1)S(1)} collective-permute-done((bf16[48,512]{1,0:T(8,128)(2,1)S(1)}, bf16[48,512]{1,0:T(8,128)(2,1)S(1)}, u32[]{:S(2)}, u32[]{:S(2)}) %collective-permute-start.1) | collective-permute-done | bytes 49184 | tf_op jit(solution)/shard_map/ppermute | solution.py:311
  55.1 6.3 %collective-permute-start.6 = (bf16[48,512]{1,0:T(8,128)(2,1)S(1)}, bf16[48,512]{1,0:T(8,128)(2,1)S(1)}, u32[]{:S(2)}, u32[]{:S(2)}) collective-permute-start(bf16[48,512]{1,0:T(8,128)(2,1)S(1)} %get-tuple-element.33), channel_id=1, source_target_pairs={{0,144},{16,128},{32,176},{48,160},{64,208},{80,192},{96,240},{112... | collective-permute-start | bytes 147464 | tf_op jit(solution)/shard_map/ppermute | solution.py:311
  61.4 0.4 collective-permute-done.2.refs_3_
  61.8 0.0 collective-permute-start.7
  61.9 0.0 collective-permute-done.3.refs_4_
  61.9 1.6 %collective-permute-start.8 = (bf16[48,512]{1,0:T(8,128)(2,1)S(1)}, bf16[48,512]{1,0:T(8,128)(2,1)S(1)}, u32[]{:S(2)}, u32[]{:S(2)}) collective-permute-start(bf16[48,512]{1,0:T(8,128)(2,1)S(1)} %get-tuple-element.35), channel_id=1, source_target_pairs={{0,80},{16,64},{32,112},{48,96},{64,144},{80,128},{96,176},{112,16... | collective-permute-start | bytes 147464 | tf_op jit(solution)/shard_map/ppermute | solution.py:311
  63.4 2.1 %collective-permute-start.9 = (bf16[48,512]{1,0:T(8,128)(2,1)S(1)}, bf16[48,512]{1,0:T(8,128)(2,1)S(1)}, u32[]{:S(2)}, u32[]{:S(2)}) collective-permute-start(bf16[48,512]{1,0:T(8,128)(2,1)S(1)} %get-tuple-element.36), channel_id=1, source_target_pairs={{0,192},{16,208},{32,224},{48,240},{64,0},{80,16},{96,32},{112,48}... | collective-permute-start | bytes 147464 | tf_op jit(solution)/shard_map/ppermute | solution.py:311
  65.5 1.9 %shard_map.92.target.refs_16_ = f32[48,384]{1,0:T(8,128)} custom-call(s32[1]{0:T(128)} %bitcast.me, bf16[768,768]{1,0:T(8,128)(2,1)S(1)} %get-tuple-element.42.pick, bf16[768,384]{1,0:T(8,128)(2,1)} %targets.1), custom_call_target="tpu_custom_call" | custom-call | flops 10000000 | tf_op jit(solution)/shard_map/pallas_call | solution.py:312
  67.4 2.8 %collective-permute-start.10 = (bf16[48,512]{1,0:T(8,128)(2,1)S(1)}, bf16[48,512]{1,0:T(8,128)(2,1)S(1)}, u32[]{:S(2)}, u32[]{:S(2)}) collective-permute-start(bf16[48,512]{1,0:T(8,128)(2,1)S(1)} %get-tuple-element.37), channel_id=1, source_target_pairs={{0,208},{16,192},{32,240},{48,224},{64,16},{80,0},{96,48},{112,32}... | collective-permute-start | bytes 147464 | tf_op jit(solution)/shard_map/ppermute | solution.py:311
  70.3 2.4 %collective-permute-start.11 = (bf16[48,512]{1,0:T(8,128)(2,1)S(1)}, bf16[48,512]{1,0:T(8,128)(2,1)}, u32[]{:S(2)}, u32[]{:S(2)}) collective-permute-start(bf16[48,512]{1,0:T(8,128)(2,1)S(1)} %get-tuple-element.38), channel_id=1, source_target_pairs={{0,32},{16,48},{32,64},{48,80},{64,96},{80,112},{96,128},{112,144}... | collective-permute-start | bytes 147464 | tf_op jit(solution)/shard_map/ppermute | solution.py:311
  72.7 0.0 collective-permute-done.7.refs_8_
  72.7 0.0 collective-permute-start.12
  72.7 0.9 collective-permute-start.13
  73.7 2.1 %collective-permute-start.14 = (bf16[48,512]{1,0:T(8,128)(2,1)S(1)}, bf16[48,512]{1,0:T(8,128)(2,1)}, u32[]{:S(2)}, u32[]{:S(2)}) collective-permute-start(bf16[48,512]{1,0:T(8,128)(2,1)S(1)} %get-tuple-element.41), channel_id=1, source_target_pairs={{0,240},{16,224},{32,16},{48,0},{64,48},{80,32},{96,80},{112,64},{... | collective-permute-start | bytes 147464 | tf_op jit(solution)/shard_map/ppermute | solution.py:311
  75.8 16.5 %shard_map.94 = (f32[32,512]{1,0:T(8,128)}, bf16[512,1024]{1,0:T(8,128)(2,1)S(1)}, bf16[512,1024]{1,0:T(8,128)(2,1)S(1)}, bf16[1024,384]{1,0:T(8,128)(2,1)S(1)}) custom-call(bf16[1536,512]{1,0:T(8,128)(2,1)S(1)} %bitcast.3, f32[48,384]{1,0:T(8,128)} %shard_map.92.target.refs_16_, bf16[512,1024]{1,0:T(8,128)(2,1)} %w_gate.1, bf16[512,1024]{1,0:T(8,128)(2,1)} %w_up.1, ...), custom_call_target="tpu_custom_call" | custom-call | flops 10000000000 | tf_op jit(solution)/shard_map/pallas_call | solution.py:317
  92.3 0.0 collective-permute-done.10.refs_11_
  92.3 0.0 collective-permute-done.11.refs_12_
  92.3 8.7 %shard_map.95 = f32[16,16,128]{2,1,0:T(8,128)S(1)} custom-call(bf16[48,512]{1,0:T(8,128)(2,1)S(1)} %copy-done.1, bf16[48,512]{1,0:T(8,128)(2,1)S(1)} %collective-permute-done.refs_1_, bf16[48,512]{1,0:T(8,128)(2,1)S(1)} %collective-permute-done.1.refs_2_, bf16[48,512]{1,0:T(8,128)(2,1)S(1)} %collective-permute-done.2.refs_3_, ...), custom_call_target="tpu_custom_call" | custom-call | flops 5000000000 | tf_op jit(solution)/shard_map/pallas_call | solution.py:327
  101.1 12.9 %all_to_all.10.arrived = f32[16,16,128]{2,1,0:T(8,128)S(1)} all-to-all(f32[16,16,128]{2,1,0:T(8,128)S(1)} %shard_map.95), channel_id=1, replica_groups=mesh['member'=16,'space'=16] {'member'}, dimensions={0} | all-to-all | bytes 262144 | tf_op jit(solution)/shard_map/all_to_all | solution.py:330
  114.0 1.0 shard_map.96
  (12 shorter events, 0.0 us)
Async XLA Ops:
  5.3 70.5 %all-to-all-start = ((bf16[16,96,512]{2,1,0:T(8,128)(2,1)}), bf16[16,96,512]{2,1,0:T(8,128)(2,1)S(1)}, u32[]{:S(2)}, u32[]{:S(2)}) async-start(bf16[16,96,512]{2,1,0:T(8,128)(2,1)} %shard_map.93), calls=%async_computation | async-start | bytes 3145728 | tf_op jit(solution)/shard_map/all_to_all | solution.py:298
  18.1 0.6 copy-start
  18.7 9.8 %collective-permute-start = (bf16[48,512]{1,0:T(8,128)(2,1)S(1)}, bf16[48,512]{1,0:T(8,128)(2,1)S(1)}, u32[]{:S(2)}, u32[]{:S(2)}) collective-permute-start(bf16[48,512]{1,0:T(8,128)(2,1)S(1)} %get-tuple-element.27), channel_id=1, source_target_pairs={{0,16},{16,0},{32,48},{48,32},{64,80},{80,64},{96,112},{112,96},{1... | collective-permute-start | bytes 147464 | tf_op jit(solution)/shard_map/ppermute | solution.py:311
  18.8 36.3 %collective-permute-start.1 = (bf16[48,512]{1,0:T(8,128)(2,1)S(1)}, bf16[48,512]{1,0:T(8,128)(2,1)S(1)}, u32[]{:S(2)}, u32[]{:S(2)}) collective-permute-start(bf16[48,512]{1,0:T(8,128)(2,1)S(1)} %get-tuple-element.28), channel_id=1, source_target_pairs={{0,96},{16,112},{32,128},{48,144},{64,160},{80,176},{96,192},{112,... | collective-permute-start | bytes 147464 | tf_op jit(solution)/shard_map/ppermute | solution.py:311
  22.3 39.6 %collective-permute-start.2 = (bf16[48,512]{1,0:T(8,128)(2,1)S(1)}, bf16[48,512]{1,0:T(8,128)(2,1)S(1)}, u32[]{:S(2)}, u32[]{:S(2)}) collective-permute-start(bf16[48,512]{1,0:T(8,128)(2,1)S(1)} %get-tuple-element.29), channel_id=1, source_target_pairs={{0,112},{16,96},{32,144},{48,128},{64,176},{80,160},{96,208},{112,... | collective-permute-start | bytes 147464 | tf_op jit(solution)/shard_map/ppermute | solution.py:311
  25.0 36.9 %collective-permute-start.3 = (bf16[48,512]{1,0:T(8,128)(2,1)S(1)}, bf16[48,512]{1,0:T(8,128)(2,1)S(1)}, u32[]{:S(2)}, u32[]{:S(2)}) collective-permute-start(bf16[48,512]{1,0:T(8,128)(2,1)S(1)} %get-tuple-element.30), channel_id=1, source_target_pairs={{0,160},{16,176},{32,192},{48,208},{64,224},{80,240},{96,0},{112,1... | collective-permute-start | bytes 147464 | tf_op jit(solution)/shard_map/ppermute | solution.py:311
  27.0 36.4 %collective-permute-start.4 = (bf16[48,512]{1,0:T(8,128)(2,1)S(1)}, bf16[48,512]{1,0:T(8,128)(2,1)S(1)}, u32[]{:S(2)}, u32[]{:S(2)}) collective-permute-start(bf16[48,512]{1,0:T(8,128)(2,1)S(1)} %get-tuple-element.31), channel_id=1, source_target_pairs={{0,176},{16,160},{32,208},{48,192},{64,240},{80,224},{96,16},{112,... | collective-permute-start | bytes 147464 | tf_op jit(solution)/shard_map/ppermute | solution.py:311
  28.5 38.9 %collective-permute-start.5 = (bf16[48,512]{1,0:T(8,128)(2,1)S(1)}, bf16[48,512]{1,0:T(8,128)(2,1)S(1)}, u32[]{:S(2)}, u32[]{:S(2)}) collective-permute-start(bf16[48,512]{1,0:T(8,128)(2,1)S(1)} %get-tuple-element.32), channel_id=1, source_target_pairs={{0,128},{16,144},{32,160},{48,176},{64,192},{80,208},{96,224},{112... | collective-permute-start | bytes 147464 | tf_op jit(solution)/shard_map/ppermute | solution.py:311
  55.1 15.1 %collective-permute-start.6 = (bf16[48,512]{1,0:T(8,128)(2,1)S(1)}, bf16[48,512]{1,0:T(8,128)(2,1)S(1)}, u32[]{:S(2)}, u32[]{:S(2)}) collective-permute-start(bf16[48,512]{1,0:T(8,128)(2,1)S(1)} %get-tuple-element.33), channel_id=1, source_target_pairs={{0,144},{16,128},{32,176},{48,160},{64,208},{80,192},{96,240},{112... | collective-permute-start | bytes 147464 | tf_op jit(solution)/shard_map/ppermute | solution.py:311
  61.8 10.9 %collective-permute-start.7 = (bf16[48,512]{1,0:T(8,128)(2,1)S(1)}, bf16[48,512]{1,0:T(8,128)(2,1)S(1)}, u32[]{:S(2)}, u32[]{:S(2)}) collective-permute-start(bf16[48,512]{1,0:T(8,128)(2,1)S(1)} %get-tuple-element.34), channel_id=1, source_target_pairs={{0,64},{16,80},{32,96},{48,112},{64,128},{80,144},{96,160},{112,17... | collective-permute-start | bytes 147464 | tf_op jit(solution)/shard_map/ppermute | solution.py:311
  61.9 10.8 %collective-permute-start.8 = (bf16[48,512]{1,0:T(8,128)(2,1)S(1)}, bf16[48,512]{1,0:T(8,128)(2,1)S(1)}, u32[]{:S(2)}, u32[]{:S(2)}) collective-permute-start(bf16[48,512]{1,0:T(8,128)(2,1)S(1)} %get-tuple-element.35), channel_id=1, source_target_pairs={{0,80},{16,64},{32,112},{48,96},{64,144},{80,128},{96,176},{112,16... | collective-permute-start | bytes 147464 | tf_op jit(solution)/shard_map/ppermute | solution.py:311
  63.4 10.2 %collective-permute-start.9 = (bf16[48,512]{1,0:T(8,128)(2,1)S(1)}, bf16[48,512]{1,0:T(8,128)(2,1)S(1)}, u32[]{:S(2)}, u32[]{:S(2)}) collective-permute-start(bf16[48,512]{1,0:T(8,128)(2,1)S(1)} %get-tuple-element.36), channel_id=1, source_target_pairs={{0,192},{16,208},{32,224},{48,240},{64,0},{80,16},{96,32},{112,48}... | collective-permute-start | bytes 147464 | tf_op jit(solution)/shard_map/ppermute | solution.py:311
  67.4 24.8 %collective-permute-start.10 = (bf16[48,512]{1,0:T(8,128)(2,1)S(1)}, bf16[48,512]{1,0:T(8,128)(2,1)S(1)}, u32[]{:S(2)}, u32[]{:S(2)}) collective-permute-start(bf16[48,512]{1,0:T(8,128)(2,1)S(1)} %get-tuple-element.37), channel_id=1, source_target_pairs={{0,208},{16,192},{32,240},{48,224},{64,16},{80,0},{96,48},{112,32}... | collective-permute-start | bytes 147464 | tf_op jit(solution)/shard_map/ppermute | solution.py:311
  70.3 22.0 %collective-permute-start.11 = (bf16[48,512]{1,0:T(8,128)(2,1)S(1)}, bf16[48,512]{1,0:T(8,128)(2,1)}, u32[]{:S(2)}, u32[]{:S(2)}) collective-permute-start(bf16[48,512]{1,0:T(8,128)(2,1)S(1)} %get-tuple-element.38), channel_id=1, source_target_pairs={{0,32},{16,48},{32,64},{48,80},{64,96},{80,112},{96,128},{112,144}... | collective-permute-start | bytes 147464 | tf_op jit(solution)/shard_map/ppermute | solution.py:311
  72.7 19.6 %collective-permute-start.12 = (bf16[48,512]{1,0:T(8,128)(2,1)S(1)}, bf16[48,512]{1,0:T(8,128)(2,1)}, u32[]{:S(2)}, u32[]{:S(2)}) collective-permute-start(bf16[48,512]{1,0:T(8,128)(2,1)S(1)} %get-tuple-element.39), channel_id=1, source_target_pairs={{0,48},{16,32},{32,80},{48,64},{64,112},{80,96},{96,144},{112,128}... | collective-permute-start | bytes 147464 | tf_op jit(solution)/shard_map/ppermute | solution.py:311
  72.7 19.6 %collective-permute-start.13 = (bf16[48,512]{1,0:T(8,128)(2,1)S(1)}, bf16[48,512]{1,0:T(8,128)(2,1)}, u32[]{:S(2)}, u32[]{:S(2)}) collective-permute-start(bf16[48,512]{1,0:T(8,128)(2,1)S(1)} %get-tuple-element.40), channel_id=1, source_target_pairs={{0,224},{16,240},{32,0},{48,16},{64,32},{80,48},{96,64},{112,80},{... | collective-permute-start | bytes 147464 | tf_op jit(solution)/shard_map/ppermute | solution.py:311
  73.7 18.7 %collective-permute-start.14 = (bf16[48,512]{1,0:T(8,128)(2,1)S(1)}, bf16[48,512]{1,0:T(8,128)(2,1)}, u32[]{:S(2)}, u32[]{:S(2)}) collective-permute-start(bf16[48,512]{1,0:T(8,128)(2,1)S(1)} %get-tuple-element.41), channel_id=1, source_target_pairs={{0,240},{16,224},{32,16},{48,0},{64,48},{80,32},{96,80},{112,64},{... | collective-permute-start | bytes 147464 | tf_op jit(solution)/shard_map/ppermute | solution.py:311
  75.8 16.6 %copy-start.1 = (bf16[48,512]{1,0:T(8,128)(2,1)S(1)}, bf16[48,512]{1,0:T(8,128)(2,1)}, u32[]{:S(2)}) copy-start(bf16[48,512]{1,0:T(8,128)(2,1)} %copy-done) | copy-start | bytes 147460

commit v2 on v1

--- a/solution.py
+++ b/solution.py
@@ -17,7 +17,7 @@
 LOCAL = 3
 MEMBERS = 48
 Z = 8
-OFFSETS = tuple((dz, dc) for dz in (0, 3, 5, 4, 2, 6, 1, 7) for dc in (0, 1))
+OFFSETS = tuple((dz, dc) for dz in (1, 7, 3, 5, 4, 2, 6, 0) for dc in (0, 1))
 CHUNKS = (32, 16)
 STARTS = (0, 32)
 SCALE = float(PIECE * OUT) ** 0.5
@@ -51,8 +51,8 @@
 def columns_of(order):
     eye = lax.broadcasted_iota(jnp.int32, (128, 128), 0) == lax.broadcasted_iota(jnp.int32, (128, 128), 1)
     found = []
-    for b in range(order.shape[1] // 128):
-        row = order[:, 128 * b : 128 * b + 128].astype(F32)
+    for b in range(order.shape[0] // 128):
+        row = order[pl.ds(128 * b, 128)].reshape(1, 128).astype(F32)
         found.append(jnp.sum(jnp.where(eye, row, 0.0), axis=1, keepdims=True).astype(jnp.int32))
     return found
 
@@ -74,7 +74,9 @@
             send[d, m * count : (m + 1) * count, :] = moved[d * count : (d + 1) * count]
 
 
-def load_state(seeds, latents, perturbation, table, seeds_here, latents_here, here, table_here, sems):
+def load_state(order, seeds, latents, perturbation, table, order_here, seeds_here, latents_here, here, table_here, sems):
+    first = pltpu.make_async_copy(order, order_here, sems.at[3 + LOCAL])
+    first.start()
     copies = [
         pltpu.make_async_copy(seeds, seeds_here, sems.at[0]),
         pltpu.make_async_copy(table, table_here, sems.at[1]),
@@ -82,6 +84,7 @@
     ] + [pltpu.make_async_copy(perturbation.at[m], here.at[m], sems.at[3 + m]) for m in range(LOCAL)]
     for copy in copies:
         copy.start()
+    first.wait()
 
     def noisy(m):
         if m == 0:
@@ -94,22 +97,16 @@
     return noisy
 
 
-def early_kernel(order, seeds, latents, perturbation, table, send, *state):
-    noisy = load_state(seeds, latents, perturbation, table, *state)
-    picked = one_hot(columns_of(order[...]), STARTS[0], CHUNKS[0], latents.shape[0])
-    move(noisy, picked, send, CHUNKS[0])
-
-
-def late_kernel(me, order, seeds, latents, perturbation, table, *rest):
-    sends, pick, state = rest[:GROUPS], rest[GROUPS], rest[GROUPS + 1 :]
-    noisy = load_state(seeds, latents, perturbation, table, *state)
-    pick[...] = one_hot(columns_of(order[...]), 0, MINE, latents.shape[0])
+def early_kernel(me, order, seeds, latents, perturbation, table, *rest):
+    sends, state, pick = rest[:GROUPS], rest[GROUPS:-1], rest[-1]
+    noisy = load_state(order, seeds, latents, perturbation, table, *state)
+    count = CHUNKS[0]
+    pick[...] = one_hot(columns_of(state[0]), STARTS[0], count, latents.shape[0])
     z, core = me[0] // 2, lax.rem(me[0], 2)
-    count = CHUNKS[1]
     parts = []
     for dz, dc in OFFSETS:
         there = lax.rem(z + dz, Z) * 2 + (1 - core if dc else core)
-        parts.append(pick[pl.ds(pl.multiple_of(there * MINE + STARTS[1], 16), count), :])
+        parts.append(pick[pl.ds(pl.multiple_of(there * count, 16), count), :])
     picked = jnp.concatenate(parts, axis=0)
     for m in range(LOCAL):
         moved = dot(picked, noisy(m)).astype(BF16)
@@ -117,8 +114,18 @@
             send[m * count : (m + 1) * count, :] = moved[k * count : (k + 1) * count]
 
 
-def target_kernel(me, pick, targets, my_targets):
+def late_kernel(order, seeds, latents, perturbation, table, send, pick, *state):
+    noisy = load_state(order, seeds, latents, perturbation, table, *state)
+    columns = columns_of(state[0])
+    pick[...] = one_hot(columns, 0, MINE, latents.shape[0])
+    move(noisy, one_hot(columns, STARTS[1], CHUNKS[1], latents.shape[0]), send, CHUNKS[1])
+
+
+def target_kernel(me, pick, targets, w_gate, w_up, lowering, my_targets, gate_here, up_here, low_here):
     my_targets[...] = dot(pick[pl.ds(pl.multiple_of(me[0] * MINE, 16), MINE), :], targets[...])
+    gate_here[...] = w_gate[...]
+    up_here[...] = w_up[...]
+    low_here[...] = lowering[...]
 
 
 def score(forecast, cotangent, target, p, gap_rows):
@@ -204,33 +211,36 @@
     return both[:count] + both[count : 2 * count] + both[2 * count :]
 
 
-def first_kernel(noisy, target, w_gate, w_up, lowering, out, gate_here, up_here, low_here, *state):
-    here, sem, sems = state[-3:]
+def first_kernel(*refs):
+    gathered, (target, w_gate, w_up, lowering, out), state = refs[:GROUPS], refs[GROUPS : GROUPS + 5], refs[GROUPS + 5 :]
+    here, sem, noisy, sems = state[-4:]
+    size = LOCAL * CHUNKS[0]
+    copies = [
+        pltpu.make_async_copy(part, noisy.at[pl.ds(k * size, size)], sems.at[k]) for k, part in enumerate(gathered)
+    ]
+    for copy in copies:
+        copy.start()
+    for copy in copies:
+        copy.wait()
+    here[...] = network(noisy, target, w_gate, w_up, lowering, state, CHUNKS[0], STARTS[0])
+    copy = pltpu.make_async_copy(here, out, sem)
+    copy.start()
+    copy.wait()
+
+
+def last_kernel(noisy, target, w_gate, w_up, lowering, earlier, out, *state):
+    here, sem, gate_here, up_here, low_here, sems = state[-6:]
     copies = [
         pltpu.make_async_copy(w_gate, gate_here, sems.at[0]),
         pltpu.make_async_copy(w_up, up_here, sems.at[1]),
         pltpu.make_async_copy(lowering, low_here, sems.at[2]),
+        pltpu.make_async_copy(earlier, here, sem),
     ]
     for copy in copies:
         copy.start()
     for copy in copies:
         copy.wait()
-    here[...] = network(noisy, target, gate_here, up_here, low_here, state, CHUNKS[0], STARTS[0])
-    copy = pltpu.make_async_copy(here, out, sem)
-    copy.start()
-    copy.wait()
-
-
-def last_kernel(*refs):
-    gathered, (target, w_gate, w_up, lowering, earlier, out), state = refs[:GROUPS], refs[GROUPS : GROUPS + 6], refs[GROUPS + 6 :]
-    here, sem, noisy = state[-3:]
-    copy = pltpu.make_async_copy(earlier, here, sem)
-    copy.start()
-    size = LOCAL * CHUNKS[1]
-    for k, part in enumerate(gathered):
-        noisy[k * size : (k + 1) * size, :] = part[...]
-    grad = network(noisy, target, w_gate, w_up, lowering, state, CHUNKS[1], STARTS[1])
-    copy.wait()
+    grad = network(noisy, target, gate_here, up_here, low_here, state, CHUNKS[1], STARTS[1])
     parts = (here[:16], here[16:], grad)
     blank = jnp.zeros((16, 32), F32)
     for d in range(GROUPS):
@@ -284,49 +294,66 @@
     )
     me = lax.axis_index("member").astype(jnp.int32).reshape(1)
     shape = jax.ShapeDtypeStruct
-    order = piece_arrangement.reshape(1, tokens)
+    order = far(piece_arrangement)
     state = (
+        pltpu.VMEM((tokens,), jnp.int32),
         pltpu.SMEM((LOCAL,), jnp.int32),
         pltpu.VMEM((tokens, LAT), BF16),
         pltpu.VMEM((LOCAL, tokens, LAT), BF16),
         pltpu.VMEM(noise_table.shape, F32),
-        pltpu.SemaphoreType.DMA((3 + LOCAL,)),
-    )
-    send0 = call(early_kernel, shape((GROUPS, LOCAL * CHUNKS[0], LAT), BF16), [VM] + [HB] * 4, VM, state, megabytes=20)(
-        order, member_seed, latents, perturbation, noise_table
-    )
-    got0 = lax.all_to_all(send0, "member", 0, 0, tiled=True)
-    *sends, pick = call(
+        pltpu.SemaphoreType.DMA((4 + LOCAL,)),
+    )
+    sends = call(
+        early_kernel,
+        [(shape if any(o) else pltpu.HBM)((LOCAL * CHUNKS[0], LAT), BF16) for o in OFFSETS],
+        [SM] + [HB] * 5,
+        [VM] * GROUPS,
+        (*state, pltpu.VMEM((GROUPS * CHUNKS[0], tokens), BF16)),
+        megabytes=16,
+    )(me, order, member_seed, latents, perturbation, noise_table)
+    got0 = []
+    for (dz, dc), send in zip(OFFSETS, sends):
+        pairs = [(2 * z + c, (z + dz) % Z * 2 + (c ^ dc)) for z in range(Z) for c in range(2)]
+        got0.append(send if dz == dc == 0 else lax.ppermute(send, "member", pairs))
+    send1, pick = call(
         late_kernel,
-        [shape((LOCAL * CHUNKS[1], LAT), BF16)] * GROUPS + [shape((tokens, tokens), BF16)],
-        [SM, VM] + [HB] * 4,
-        [VM] * (GROUPS + 1),
+        [shape((GROUPS, LOCAL * CHUNKS[1], LAT), BF16), shape((tokens, tokens), BF16)],
+        [HB] * 5,
+        [VM, VM],
         state,
         flops=10**9,
-        megabytes=20,
-    )(me, order, member_seed, latents, perturbation, noise_table)
-    got1 = []
-    for (dz, dc), send in zip(OFFSETS, sends):
-        pairs = [(2 * z + c, (z + dz) % Z * 2 + (c ^ dc)) for z in range(Z) for c in range(2)]
-        got1.append(send if dz == dc == 0 else lax.ppermute(send, "member", pairs))
-    my_targets = call(target_kernel, pltpu.HBM((MINE, OUT), F32), [SM, VM, VM], VM, flops=10**7, megabytes=4)(
-        me, pick, targets
-    )
+        megabytes=16,
+    )(order, member_seed, latents, perturbation, noise_table)
+    got1 = lax.all_to_all(send1, "member", 0, 0, tiled=True)
+    weights = tuple(far(w) for w in (w_gate, w_up, lowering_matrix))
+    my_targets, *near = call(
+        target_kernel,
+        [pltpu.HBM((MINE, OUT), F32), *(shape(w.shape, BF16) for w in weights)],
+        [SM] + [VM] * 5,
+        [VM] * 4,
+        flops=10**7,
+        megabytes=10,
+    )(me, pick, targets, *weights)
     my_targets = far(my_targets)
-    weights = tuple(far(w) for w in (w_gate, w_up, lowering_matrix))
-    earlier, *weights = call(
+    earlier = call(
         first_kernel,
-        [pltpu.HBM((CHUNKS[0], LAT), F32), *(shape(w.shape, BF16) for w in weights)],
-        [VM] + [HB] * 4,
-        [HB] + [VM] * 3,
-        (*scratch(CHUNKS[0]), pltpu.SemaphoreType.DMA((3,))),
+        pltpu.HBM((CHUNKS[0], LAT), F32),
+        [HB] * GROUPS + [HB, VM, VM, VM],
+        HB,
+        (*scratch(CHUNKS[0]), pltpu.VMEM((MEMBERS * CHUNKS[0], LAT), BF16), pltpu.SemaphoreType.DMA((GROUPS,))),
         10**10,
-        32,
-    )(got0.reshape(MEMBERS * CHUNKS[0], LAT), my_targets, *weights)
-    extra = (*scratch(CHUNKS[1]), pltpu.VMEM((MEMBERS * CHUNKS[1], LAT), BF16))
-    packed = call(
-        last_kernel, shape((GROUPS, 16, 128), F32), [VM] * GROUPS + [HB, VM, VM, VM, HB], VM, extra, 5 * 10**9, 24
-    )(*got1, my_targets, *weights, far(earlier))
+        30,
+    )(*(far(part) for part in got0), my_targets, *near)
+    extra = (
+        *scratch(CHUNKS[1]),
+        pltpu.VMEM((LAT, HID), BF16),
+        pltpu.VMEM((LAT, HID), BF16),
+        pltpu.VMEM((HID, OUT), BF16),
+        pltpu.SemaphoreType.DMA((3,)),
+    )
+    packed = call(last_kernel, shape((GROUPS, 16, 128), F32), [VM] + [HB] * 5, VM, extra, 5 * 10**9, 22)(
+        got1.reshape(MEMBERS * CHUNKS[1], LAT), my_targets, *weights, far(earlier)
+    )
     arrived = lax.all_to_all(packed, "member", 0, 0, tiled=True)
     columns = call(unpack_kernel, shape((LAT // GROUPS, tokens), F32), [VM] * 2, VM)(arrived, pick)
     return columns.T

time: 115 us -> 118 us (1.026)
  starting transfers between devices: 43.4 us -> 36.7 us
  waiting for transfers between devices: 21.7 us -> 28 us
  Pallas kernels: 35.6 us -> 37.6 us
  blocking collectives: 12.9 us -> 14.9 us
    ppermute x15, starting transfers between devices: 33.4 us -> 26.7 us  [body(): got0.append(send if dz == dc == 0 else lax.ppermute(send, 'member', pairs))]
    ppermute x15, waiting for transfers between devices: 21.7 us -> 28 us  [body(): got0.append(send if dz == dc == 0 else lax.ppermute(send, 'member', pairs))]
    pallas_call x5, Pallas kernels: 34.6 us -> 36.6 us  [the longest x1 16.3 us: body(): call(first_kernel, pltpu.HBM((CHUNKS[0], LAT), F32), [HB] * GROUPS + [HB,...]
    all_to_all x1, blocking collectives: 12.9 us -> 14.9 us  [body(): arrived = lax.all_to_all(packed, 'member', 0, 0, tiled=True)]
  transfers between devices with their start and end apart: 16 -> 16, of which waited for: 2 -> 6; matrix products, arithmetic and copies ran while one was open for 0% -> 0% of each run, Pallas kernels for 18% -> 20%
where the time goes in v2:
time: 118 us
  Pallas kernels  37.6 us (32%)
  starting transfers between devices  36.7 us (31%)
  waiting for transfers between devices  28 us (24%)
  blocking collectives  14.9 us (13%)
    ppermute x15, waiting for transfers between devices, body(): got0.append(send if dz == dc == 0 else lax.ppermute(send, 'member', pairs))  28 us
    ppermute x15, starting transfers between devices, body(): got0.append(send if dz == dc == 0 else lax.ppermute(send, 'member', pairs))  26.7 us
    pallas_call x1, Pallas kernels, body(): call(first_kernel, pltpu.HBM((CHUNKS[0], LAT), F32), [HB] * GROUPS + [HB,...  16.3 us
    all_to_all x1, blocking collectives, body(): arrived = lax.all_to_all(packed, 'member', 0, 0, tiled=True)  14.9 us
    all_to_all x1, starting transfers between devices, body(): got1 = lax.all_to_all(send1, 'member', 0, 0, tiled=True)  9.98 us
    pallas_call x1, Pallas kernels, body(): call(last_kernel, shape((GROUPS, 16, 128), F32), [VM] + [HB] * 5, VM, ext...  9.52 us
    pallas_call x1, Pallas kernels, body(): call(early_kernel, [(shape if any(o) else pltpu.HBM)((LOCAL * CHUNKS[0],...  4.04 us
    pallas_call x1, Pallas kernels, body(): call(late_kernel, [shape((GROUPS, LOCAL * CHUNKS[1], LAT), BF16), shape((...  3.78 us
  transfers between devices with their start and end apart: 16, of which 6 were waited for; matrix products, arithmetic and copies ran while one was open for 0% of the time, Pallas kernels for 20%

profile of v2, /device:TPU:1, one launch (start us, length us, event | category | flops | bytes accessed | tf_op | source)
XLA Modules:
  0.0 118.1 jit_solution(10098551159923016336)
XLA Ops:
  0.0 3.8 %shard_map.91 = (bf16[16,48,512]{2,1,0:T(8,128)(2,1)}, bf16[768,768]{1,0:T(8,128)(2,1)S(1)}) custom-call(s32[768]{0:T(1024)} %order.3, s32[3]{0:T(128)} %seeds.3, bf16[768,512]{1,0:T(8,128)(2,1)} %latents.3, bf16[3,768,512]{2,1,0:T(8,128)(2,1)} %perturbation.3, f32[64,512]{1,0:T(8,128)} %table.3), custom_call_target="tpu_custom_call" | custom-call | flops 1000000000 | tf_op jit(solution)/shard_map/pallas_call | solution.py:318
  3.8 10.0 %all-to-all-start = ((bf16[16,48,512]{2,1,0:T(8,128)(2,1)}), bf16[16,48,512]{2,1,0:T(8,128)(2,1)S(1)}, u32[]{:S(2)}, u32[]{:S(2)}) async-start(bf16[16,48,512]{2,1,0:T(8,128)(2,1)} %get-tuple-element.27), calls=%async_computation | async-start | bytes 1572864 | tf_op jit(solution)/shard_map/all_to_all | solution.py:327
  13.8 4.0 %shard_map.93 = (bf16[96,512]{1,0:T(8,128)(2,1)S(1)}, bf16[96,512]{1,0:T(8,128)(2,1)S(1)}, bf16[96,512]{1,0:T(8,128)(2,1)S(1)}, bf16[96,512]{1,0:T(8,128)(2,1)S(...) custom-call(s32[1]{0:T(128)} %bitcast.1.me, ...), custom_call_target="tpu_custom_call" | custom-call | tf_op jit(solution)/shard_map/pallas_call | solution.py:306
  17.8 1.4 %collective-permute-start = (bf16[96,512]{1,0:T(8,128)(2,1)S(1)}, bf16[96,512]{1,0:T(8,128)(2,1)S(1)}, u32[]{:S(2)}, u32[]{:S(2)}) collective-permute-start(bf16[96,512]{1,0:T(8,128)(2,1)S(1)} %get-tuple-element.30), channel_id=1, source_target_pairs={{0,32},{16,48},{32,64},{48,80},{64,96},{80,112},{96,128},{112,144}... | collective-permute-start | bytes 294920 | tf_op jit(solution)/shard_map/ppermute | solution.py:317
  19.2 1.7 %collective-permute-start.1 = (bf16[96,512]{1,0:T(8,128)(2,1)S(1)}, bf16[96,512]{1,0:T(8,128)(2,1)S(1)}, u32[]{:S(2)}, u32[]{:S(2)}) collective-permute-start(bf16[96,512]{1,0:T(8,128)(2,1)S(1)} %get-tuple-element.31), channel_id=1, source_target_pairs={{0,48},{16,32},{32,80},{48,64},{64,112},{80,96},{96,144},{112,128}... | collective-permute-start | bytes 294920 | tf_op jit(solution)/shard_map/ppermute | solution.py:317
  21.0 1.5 %collective-permute-start.2 = (bf16[96,512]{1,0:T(8,128)(2,1)S(1)}, bf16[96,512]{1,0:T(8,128)(2,1)S(1)}, u32[]{:S(2)}, u32[]{:S(2)}) collective-permute-start(bf16[96,512]{1,0:T(8,128)(2,1)S(1)} %get-tuple-element.32), channel_id=1, source_target_pairs={{0,224},{16,240},{32,0},{48,16},{64,32},{80,48},{96,64},{112,80},{... | collective-permute-start | bytes 294920 | tf_op jit(solution)/shard_map/ppermute | solution.py:317
  22.5 0.3 collective-permute-start.3
  22.8 2.7 %collective-permute-start.4 = (bf16[96,512]{1,0:T(8,128)(2,1)S(1)}, bf16[96,512]{1,0:T(8,128)(2,1)S(1)}, u32[]{:S(2)}, u32[]{:S(2)}) collective-permute-start(bf16[96,512]{1,0:T(8,128)(2,1)S(1)} %get-tuple-element.34), channel_id=1, source_target_pairs={{0,96},{16,112},{32,128},{48,144},{64,160},{80,176},{96,192},{112,... | collective-permute-start | bytes 294920 | tf_op jit(solution)/shard_map/ppermute | solution.py:317
  25.5 10.5 %collective-permute-done.refs_0_ = bf16[96,512]{1,0:T(8,128)(2,1)S(1)} collective-permute-done((bf16[96,512]{1,0:T(8,128)(2,1)S(1)}, bf16[96,512]{1,0:T(8,128)(2,1)S(1)}, u32[]{:S(2)}, u32[]{:S(2)}) %collective-permute-start) | collective-permute-done | bytes 98336 | tf_op jit(solution)/shard_map/ppermute | solution.py:317
  36.0 2.5 %collective-permute-start.5 = (bf16[96,512]{1,0:T(8,128)(2,1)S(1)}, bf16[96,512]{1,0:T(8,128)(2,1)S(1)}, u32[]{:S(2)}, u32[]{:S(2)}) collective-permute-start(bf16[96,512]{1,0:T(8,128)(2,1)S(1)} %get-tuple-element.35), channel_id=1, source_target_pairs={{0,112},{16,96},{32,144},{48,128},{64,176},{80,160},{96,208},{112,... | collective-permute-start | bytes 294920 | tf_op jit(solution)/shard_map/ppermute | solution.py:317
  38.4 1.0 collective-permute-done.1.refs_1_
  39.4 5.7 %collective-permute-start.6 = (bf16[96,512]{1,0:T(8,128)(2,1)S(1)}, bf16[96,512]{1,0:T(8,128)(2,1)S(1)}, u32[]{:S(2)}, u32[]{:S(2)}) collective-permute-start(bf16[96,512]{1,0:T(8,128)(2,1)S(1)} %get-tuple-element.36), channel_id=1, source_target_pairs={{0,160},{16,176},{32,192},{48,208},{64,224},{80,240},{96,0},{112,1... | collective-permute-start | bytes 294920 | tf_op jit(solution)/shard_map/ppermute | solution.py:317
  45.1 0.0 collective-permute-done.3.refs_3_
  45.1 1.2 %collective-permute-start.8 = (bf16[96,512]{1,0:T(8,128)(2,1)S(1)}, bf16[96,512]{1,0:T(8,128)(2,1)S(1)}, u32[]{:S(2)}, u32[]{:S(2)}) collective-permute-start(bf16[96,512]{1,0:T(8,128)(2,1)S(1)} %get-tuple-element.38), channel_id=1, source_target_pairs={{0,128},{16,144},{32,160},{48,176},{64,192},{80,208},{96,224},{112... | collective-permute-start | bytes 294920 | tf_op jit(solution)/shard_map/ppermute | solution.py:317
  46.3 0.0 collective-permute-done.4.refs_4_
  46.3 4.8 %collective-permute-start.9 = (bf16[96,512]{1,0:T(8,128)(2,1)S(1)}, bf16[96,512]{1,0:T(8,128)(2,1)S(1)}, u32[]{:S(2)}, u32[]{:S(2)}) collective-permute-start(bf16[96,512]{1,0:T(8,128)(2,1)S(1)} %get-tuple-element.39), channel_id=1, source_target_pairs={{0,144},{16,128},{32,176},{48,160},{64,208},{80,192},{96,240},{112... | collective-permute-start | bytes 294920 | tf_op jit(solution)/shard_map/ppermute | solution.py:317
  51.1 1.8 %collective-permute-done.5.refs_5_ = bf16[96,512]{1,0:T(8,128)(2,1)S(1)} collective-permute-done((bf16[96,512]{1,0:T(8,128)(2,1)S(1)}, bf16[96,512]{1,0:T(8,128)(2,1)S(1)}, u32[]{:S(2)}, u32[]{:S(2)}) %collective-permute-start.5) | collective-permute-done | bytes 98336 | tf_op jit(solution)/shard_map/ppermute | solution.py:317
  52.9 0.0 collective-permute-start.10
  52.9 0.0 collective-permute-done.6.refs_6_
  52.9 4.7 %collective-permute-start.11 = (bf16[96,512]{1,0:T(8,128)(2,1)S(1)}, bf16[96,512]{1,0:T(8,128)(2,1)S(1)}, u32[]{:S(2)}, u32[]{:S(2)}) collective-permute-start(bf16[96,512]{1,0:T(8,128)(2,1)S(1)} %get-tuple-element.41), channel_id=1, source_target_pairs={{0,80},{16,64},{32,112},{48,96},{64,144},{80,128},{96,176},{112,16... | collective-permute-start | bytes 294920 | tf_op jit(solution)/shard_map/ppermute | solution.py:317
  57.6 8.0 %collective-permute-done.7.refs_7_ = bf16[96,512]{1,0:T(8,128)(2,1)S(1)} collective-permute-done((bf16[96,512]{1,0:T(8,128)(2,1)S(1)}, bf16[96,512]{1,0:T(8,128)(2,1)S(1)}, u32[]{:S(2)}, u32[]{:S(2)}) %collective-permute-start.7) | collective-permute-done | bytes 98336 | tf_op jit(solution)/shard_map/ppermute | solution.py:317
  65.6 0.1 collective-permute-start.13
  65.7 0.1 collective-permute-start.14
  65.8 3.0 %shard_map.92 = (f32[48,384]{1,0:T(8,128)}, bf16[512,1024]{1,0:T(8,128)(2,1)S(1)}, bf16[512,1024]{1,0:T(8,128)(2,1)S(1)}, bf16[1024,384]{1,0:T(8,128)(2,1)S(1)}) custom-call(s32[1]{0:T(128)} %bitcast.1.me, bf16[768,768]{1,0:T(8,128)(2,1)S(1)} %get-tuple-element.28.pick, bf16[768,384]{1,0:T(8,128)(2,1)} %targets.1, bf16[512,1024]{1,0:T(8,128)(2,1)} %w_gate.3, ...), custom_call_target="tpu_custom_call" | custom-call | flops 10000000 | tf_op jit(solution)/shard_map/pallas_call | solution.py:329
  68.9 4.5 %collective-permute-done.12.refs_12_ = bf16[96,512]{1,0:T(8,128)(2,1)S(1)} collective-permute-done((bf16[96,512]{1,0:T(8,128)(2,1)S(1)}, bf16[96,512]{1,0:T(8,128)(2,1)S(1)}, u32[]{:S(2)}, u32[]{:S(2)}) %collective-permute-start.12) | collective-permute-done | bytes 98336 | tf_op jit(solution)/shard_map/ppermute | solution.py:317
  73.4 2.3 %collective-permute-done.13.refs_13_ = bf16[96,512]{1,0:T(8,128)(2,1)S(1)} collective-permute-done((bf16[96,512]{1,0:T(8,128)(2,1)S(1)}, bf16[96,512]{1,0:T(8,128)(2,1)S(1)}, u32[]{:S(2)}, u32[]{:S(2)}) %collective-permute-start.13) | collective-permute-done | bytes 98336 | tf_op jit(solution)/shard_map/ppermute | solution.py:317
  75.8 0.5 copy-done.13
  76.3 0.0 copy-done.14
  76.3 16.3 %shard_map.94.earlier = f32[32,512]{1,0:T(8,128)} custom-call(bf16[96,512]{1,0:T(8,128)(2,1)} %copy-done, bf16[96,512]{1,0:T(8,128)(2,1)} %copy-done.1, bf16[96,512]{1,0:T(8,128)(2,1)} %copy-done.2, bf16[96,512]{1,0:T(8,128)(2,1)} %copy-done.3, bf16[96,512]{1,0:T(8,128)(2,1)} %copy-done.4, bf16[96,512]{1,0:T(8,128)(2,1)} %copy-done.5, ...), custom_call_target="tpu_custom_call" | custom-call | flops 10000000000 | tf_op jit(solution)/shard_map/pallas_call | solution.py:338
  92.7 9.5 %shard_map.95 = f32[16,16,128]{2,1,0:T(8,128)S(1)} custom-call(bf16[768,512]{1,0:T(8,128)(2,1)S(1)} %bitcast.3, f32[48,384]{1,0:T(8,128)} %get-tuple-element.29.refs_16_.target, bf16[512,1024]{1,0:T(8,128)(2,1)} %w_gate.3, bf16[512,1024]{1,0:T(8,128)(2,1)} %w_up.3, bf16[1024,384]{1,0:T(8,128)(2,1)} %lowering.3, f32[32,512]{1,0:T(8,128)} %shard_map.94.earlier), custom_call_target="tpu_custom_call" | custom-call | flops 5000000000 | tf_op jit(solution)/shard_map/pallas_call | solution.py:354
  102.2 14.9 %all_to_all.10.arrived = f32[16,16,128]{2,1,0:T(8,128)S(1)} all-to-all(f32[16,16,128]{2,1,0:T(8,128)S(1)} %shard_map.95), channel_id=1, replica_groups=mesh['member'=16,'space'=16] {'member'}, dimensions={0} | all-to-all | bytes 262144 | tf_op jit(solution)/shard_map/all_to_all | solution.py:357
  117.1 1.0 shard_map.96
  (37 shorter events, 0.1 us)
Async XLA Ops:
  3.8 88.9 %all-to-all-start = ((bf16[16,48,512]{2,1,0:T(8,128)(2,1)}), bf16[16,48,512]{2,1,0:T(8,128)(2,1)S(1)}, u32[]{:S(2)}, u32[]{:S(2)}) async-start(bf16[16,48,512]{2,1,0:T(8,128)(2,1)} %get-tuple-element.27), calls=%async_computation | async-start | bytes 1572864 | tf_op jit(solution)/shard_map/all_to_all | solution.py:327
  17.8 18.1 %collective-permute-start = (bf16[96,512]{1,0:T(8,128)(2,1)S(1)}, bf16[96,512]{1,0:T(8,128)(2,1)S(1)}, u32[]{:S(2)}, u32[]{:S(2)}) collective-permute-start(bf16[96,512]{1,0:T(8,128)(2,1)S(1)} %get-tuple-element.30), channel_id=1, source_target_pairs={{0,32},{16,48},{32,64},{48,80},{64,96},{80,112},{96,128},{112,144}... | collective-permute-start | bytes 294920 | tf_op jit(solution)/shard_map/ppermute | solution.py:317
  19.2 20.1 %collective-permute-start.1 = (bf16[96,512]{1,0:T(8,128)(2,1)S(1)}, bf16[96,512]{1,0:T(8,128)(2,1)S(1)}, u32[]{:S(2)}, u32[]{:S(2)}) collective-permute-start(bf16[96,512]{1,0:T(8,128)(2,1)S(1)} %get-tuple-element.31), channel_id=1, source_target_pairs={{0,48},{16,32},{32,80},{48,64},{64,112},{80,96},{96,144},{112,128}... | collective-permute-start | bytes 294920 | tf_op jit(solution)/shard_map/ppermute | solution.py:317
  21.0 24.1 %collective-permute-start.2 = (bf16[96,512]{1,0:T(8,128)(2,1)S(1)}, bf16[96,512]{1,0:T(8,128)(2,1)S(1)}, u32[]{:S(2)}, u32[]{:S(2)}) collective-permute-start(bf16[96,512]{1,0:T(8,128)(2,1)S(1)} %get-tuple-element.32), channel_id=1, source_target_pairs={{0,224},{16,240},{32,0},{48,16},{64,32},{80,48},{96,64},{112,80},{... | collective-permute-start | bytes 294920 | tf_op jit(solution)/shard_map/ppermute | solution.py:317
  22.5 22.6 %collective-permute-start.3 = (bf16[96,512]{1,0:T(8,128)(2,1)S(1)}, bf16[96,512]{1,0:T(8,128)(2,1)S(1)}, u32[]{:S(2)}, u32[]{:S(2)}) collective-permute-start(bf16[96,512]{1,0:T(8,128)(2,1)S(1)} %get-tuple-element.33), channel_id=1, source_target_pairs={{0,240},{16,224},{32,16},{48,0},{64,48},{80,32},{96,80},{112,64},{... | collective-permute-start | bytes 294920 | tf_op jit(solution)/shard_map/ppermute | solution.py:317
  22.8 23.5 %collective-permute-start.4 = (bf16[96,512]{1,0:T(8,128)(2,1)S(1)}, bf16[96,512]{1,0:T(8,128)(2,1)S(1)}, u32[]{:S(2)}, u32[]{:S(2)}) collective-permute-start(bf16[96,512]{1,0:T(8,128)(2,1)S(1)} %get-tuple-element.34), channel_id=1, source_target_pairs={{0,96},{16,112},{32,128},{48,144},{64,160},{80,176},{96,192},{112,... | collective-permute-start | bytes 294920 | tf_op jit(solution)/shard_map/ppermute | solution.py:317
  36.0 39.7 %copy-start = (bf16[96,512]{1,0:T(8,128)(2,1)}, bf16[96,512]{1,0:T(8,128)(2,1)S(1)}, u32[]{:S(2)}) copy-start(bf16[96,512]{1,0:T(8,128)(2,1)S(1)} %collective-permute-done.refs_0_) | copy-start | bytes 294916
  36.0 16.9 %collective-permute-start.5 = (bf16[96,512]{1,0:T(8,128)(2,1)S(1)}, bf16[96,512]{1,0:T(8,128)(2,1)S(1)}, u32[]{:S(2)}, u32[]{:S(2)}) collective-permute-start(bf16[96,512]{1,0:T(8,128)(2,1)S(1)} %get-tuple-element.35), channel_id=1, source_target_pairs={{0,112},{16,96},{32,144},{48,128},{64,176},{80,160},{96,208},{112,... | collective-permute-start | bytes 294920 | tf_op jit(solution)/shard_map/ppermute | solution.py:317
  39.4 36.3 %copy-start.1 = (bf16[96,512]{1,0:T(8,128)(2,1)}, bf16[96,512]{1,0:T(8,128)(2,1)S(1)}, u32[]{:S(2)}) copy-start(bf16[96,512]{1,0:T(8,128)(2,1)S(1)} %collective-permute-done.1.refs_1_) | copy-start | bytes 294916
  39.4 13.5 %collective-permute-start.6 = (bf16[96,512]{1,0:T(8,128)(2,1)S(1)}, bf16[96,512]{1,0:T(8,128)(2,1)S(1)}, u32[]{:S(2)}, u32[]{:S(2)}) collective-permute-start(bf16[96,512]{1,0:T(8,128)(2,1)S(1)} %get-tuple-element.36), channel_id=1, source_target_pairs={{0,160},{16,176},{32,192},{48,208},{64,224},{80,240},{96,0},{112,1... | collective-permute-start | bytes 294920 | tf_op jit(solution)/shard_map/ppermute | solution.py:317
  45.1 30.6 %copy-start.2 = (bf16[96,512]{1,0:T(8,128)(2,1)}, bf16[96,512]{1,0:T(8,128)(2,1)S(1)}, u32[]{:S(2)}) copy-start(bf16[96,512]{1,0:T(8,128)(2,1)S(1)} %collective-permute-done.2.refs_2_) | copy-start | bytes 294916
  45.1 20.5 %collective-permute-start.7 = (bf16[96,512]{1,0:T(8,128)(2,1)S(1)}, bf16[96,512]{1,0:T(8,128)(2,1)S(1)}, u32[]{:S(2)}, u32[]{:S(2)}) collective-permute-start(bf16[96,512]{1,0:T(8,128)(2,1)S(1)} %get-tuple-element.37), channel_id=1, source_target_pairs={{0,176},{16,160},{32,208},{48,192},{64,240},{80,224},{96,16},{112,... | collective-permute-start | bytes 294920 | tf_op jit(solution)/shard_map/ppermute | solution.py:317
  45.1 30.6 %copy-start.3 = (bf16[96,512]{1,0:T(8,128)(2,1)}, bf16[96,512]{1,0:T(8,128)(2,1)S(1)}, u32[]{:S(2)}) copy-start(bf16[96,512]{1,0:T(8,128)(2,1)S(1)} %collective-permute-done.3.refs_3_) | copy-start | bytes 294916
  45.1 20.5 %collective-permute-start.8 = (bf16[96,512]{1,0:T(8,128)(2,1)S(1)}, bf16[96,512]{1,0:T(8,128)(2,1)S(1)}, u32[]{:S(2)}, u32[]{:S(2)}) collective-permute-start(bf16[96,512]{1,0:T(8,128)(2,1)S(1)} %get-tuple-element.38), channel_id=1, source_target_pairs={{0,128},{16,144},{32,160},{48,176},{64,192},{80,208},{96,224},{112... | collective-permute-start | bytes 294920 | tf_op jit(solution)/shard_map/ppermute | solution.py:317
  46.3 29.4 %copy-start.4 = (bf16[96,512]{1,0:T(8,128)(2,1)}, bf16[96,512]{1,0:T(8,128)(2,1)S(1)}, u32[]{:S(2)}) copy-start(bf16[96,512]{1,0:T(8,128)(2,1)S(1)} %collective-permute-done.4.refs_4_) | copy-start | bytes 294916
  46.3 19.4 %collective-permute-start.9 = (bf16[96,512]{1,0:T(8,128)(2,1)S(1)}, bf16[96,512]{1,0:T(8,128)(2,1)S(1)}, u32[]{:S(2)}, u32[]{:S(2)}) collective-permute-start(bf16[96,512]{1,0:T(8,128)(2,1)S(1)} %get-tuple-element.39), channel_id=1, source_target_pairs={{0,144},{16,128},{32,176},{48,160},{64,208},{80,192},{96,240},{112... | collective-permute-start | bytes 294920 | tf_op jit(solution)/shard_map/ppermute | solution.py:317
  52.9 22.8 %copy-start.5 = (bf16[96,512]{1,0:T(8,128)(2,1)}, bf16[96,512]{1,0:T(8,128)(2,1)S(1)}, u32[]{:S(2)}) copy-start(bf16[96,512]{1,0:T(8,128)(2,1)S(1)} %collective-permute-done.5.refs_5_) | copy-start | bytes 294916
  52.9 16.0 %collective-permute-start.10 = (bf16[96,512]{1,0:T(8,128)(2,1)S(1)}, bf16[96,512]{1,0:T(8,128)(2,1)S(1)}, u32[]{:S(2)}, u32[]{:S(2)}) collective-permute-start(bf16[96,512]{1,0:T(8,128)(2,1)S(1)} %get-tuple-element.40), channel_id=1, source_target_pairs={{0,64},{16,80},{32,96},{48,112},{64,128},{80,144},{96,160},{112,17... | collective-permute-start | bytes 294920 | tf_op jit(solution)/shard_map/ppermute | solution.py:317
  52.9 22.8 %copy-start.6 = (bf16[96,512]{1,0:T(8,128)(2,1)}, bf16[96,512]{1,0:T(8,128)(2,1)S(1)}, u32[]{:S(2)}) copy-start(bf16[96,512]{1,0:T(8,128)(2,1)S(1)} %collective-permute-done.6.refs_6_) | copy-start | bytes 294916
  52.9 16.0 %collective-permute-start.11 = (bf16[96,512]{1,0:T(8,128)(2,1)S(1)}, bf16[96,512]{1,0:T(8,128)(2,1)S(1)}, u32[]{:S(2)}, u32[]{:S(2)}) collective-permute-start(bf16[96,512]{1,0:T(8,128)(2,1)S(1)} %get-tuple-element.41), channel_id=1, source_target_pairs={{0,80},{16,64},{32,112},{48,96},{64,144},{80,128},{96,176},{112,16... | collective-permute-start | bytes 294920 | tf_op jit(solution)/shard_map/ppermute | solution.py:317
  65.6 10.1 %copy-start.7 = (bf16[96,512]{1,0:T(8,128)(2,1)}, bf16[96,512]{1,0:T(8,128)(2,1)S(1)}, u32[]{:S(2)}) copy-start(bf16[96,512]{1,0:T(8,128)(2,1)S(1)} %collective-permute-done.7.refs_7_) | copy-start | bytes 294916
  65.6 7.8 %collective-permute-start.12 = (bf16[96,512]{1,0:T(8,128)(2,1)S(1)}, bf16[96,512]{1,0:T(8,128)(2,1)S(1)}, u32[]{:S(2)}, u32[]{:S(2)}) collective-permute-start(bf16[96,512]{1,0:T(8,128)(2,1)S(1)} %get-tuple-element.42), channel_id=1, source_target_pairs={{0,192},{16,208},{32,224},{48,240},{64,0},{80,16},{96,32},{112,48}... | collective-permute-start | bytes 294920 | tf_op jit(solution)/shard_map/ppermute | solution.py:317
  65.6 10.1 %copy-start.8 = (bf16[96,512]{1,0:T(8,128)(2,1)}, bf16[96,512]{1,0:T(8,128)(2,1)S(1)}, u32[]{:S(2)}) copy-start(bf16[96,512]{1,0:T(8,128)(2,1)S(1)} %collective-permute-done.8.refs_8_) | copy-start | bytes 294916
  65.6 10.0 %collective-permute-start.13 = (bf16[96,512]{1,0:T(8,128)(2,1)S(1)}, bf16[96,512]{1,0:T(8,128)(2,1)S(1)}, u32[]{:S(2)}, u32[]{:S(2)}) collective-permute-start(bf16[96,512]{1,0:T(8,128)(2,1)S(1)} %get-tuple-element.43), channel_id=1, source_target_pairs={{0,208},{16,192},{32,240},{48,224},{64,16},{80,0},{96,48},{112,32}... | collective-permute-start | bytes 294920 | tf_op jit(solution)/shard_map/ppermute | solution.py:317
  65.7 10.0 %copy-start.9 = (bf16[96,512]{1,0:T(8,128)(2,1)}, bf16[96,512]{1,0:T(8,128)(2,1)S(1)}, u32[]{:S(2)}) copy-start(bf16[96,512]{1,0:T(8,128)(2,1)S(1)} %collective-permute-done.9.refs_9_) | copy-start | bytes 294916
  65.7 9.9 %collective-permute-start.14 = (bf16[96,512]{1,0:T(8,128)(2,1)S(1)}, bf16[96,512]{1,0:T(8,128)(2,1)S(1)}, u32[]{:S(2)}, u32[]{:S(2)}) collective-permute-start(bf16[96,512]{1,0:T(8,128)(2,1)S(1)} %get-tuple-element.45), channel_id=1, source_target_pairs={{0,16},{16,0},{32,48},{48,32},{64,80},{80,64},{96,112},{112,96},{1... | collective-permute-start | bytes 294920 | tf_op jit(solution)/shard_map/ppermute | solution.py:317
  68.9 6.9 %copy-start.10 = (bf16[96,512]{1,0:T(8,128)(2,1)}, bf16[96,512]{1,0:T(8,128)(2,1)S(1)}, u32[]{:S(2)}) copy-start(bf16[96,512]{1,0:T(8,128)(2,1)S(1)} %collective-permute-done.10.refs_10_) | copy-start | bytes 294916
  68.9 6.9 %copy-start.11 = (bf16[96,512]{1,0:T(8,128)(2,1)}, bf16[96,512]{1,0:T(8,128)(2,1)S(1)}, u32[]{:S(2)}) copy-start(bf16[96,512]{1,0:T(8,128)(2,1)S(1)} %collective-permute-done.11.refs_11_) | copy-start | bytes 294916
  73.4 2.4 %copy-start.12 = (bf16[96,512]{1,0:T(8,128)(2,1)}, bf16[96,512]{1,0:T(8,128)(2,1)S(1)}, u32[]{:S(2)}) copy-start(bf16[96,512]{1,0:T(8,128)(2,1)S(1)} %collective-permute-done.12.refs_12_) | copy-start | bytes 294916
  75.7 0.6 copy-start.13
  75.7 0.7 copy-start.14

commit v3 on v2

--- a/solution.py
+++ b/solution.py
@@ -10,14 +10,14 @@
 HID = 1024
 OUT = 384
 PIECE = 8
-BLOCK = 256
+BLOCK = 384
 PAD = 8
 GROUPS = 16
 MINE = 48
 LOCAL = 3
 MEMBERS = 48
 Z = 8
-OFFSETS = tuple((dz, dc) for dz in (1, 7, 3, 5, 4, 2, 6, 0) for dc in (0, 1))
+OFFSETS = tuple((dz, dc) for dz in (3, 5, 4, 2, 6, 1, 7, 0) for dc in (0, 1))
 CHUNKS = (32, 16)
 STARTS = (0, 32)
 SCALE = float(PIECE * OUT) ** 0.5
@@ -132,7 +132,7 @@
     def token(r):
         at = pl.ds(p * PIECE + r, MEMBERS, stride=gap_rows)
         u = jnp.concatenate([forecast[j, at, :] for j in range(3)], axis=1)
-        return at, u, u - target[p * PIECE + r : p * PIECE + r + 1, :]
+        return at, u, u - target[r : r + 1, :]
 
     gram = jnp.zeros((MEMBERS, MEMBERS), F32)
     norm = jnp.zeros((MEMBERS, 128), F32)
@@ -185,8 +185,10 @@
                 forecast[j, to, :] = made[count * q : count * q + count, 128 * j : 128 * j + 128]
 
     copy.wait()
-    for p in range(count // PIECE):
-        score(forecast, cotangent, target_here, p, gap_rows)
+
+    @pl.loop(0, count // PIECE)
+    def _(p):
+        score(forecast, cotangent, target_here[pl.ds(pl.multiple_of(p * PIECE, PIECE), PIECE), :], p, gap_rows)
 
     token = lax.broadcasted_iota(jnp.int32, (count, block), 0)
     place = lax.broadcasted_iota(jnp.int32, (count, block), 1)

time: 118 us -> 112 us (0.949)
  waiting for transfers between devices: 28 us -> 13.1 us
  starting transfers between devices: 36.7 us -> 48.1 us
  blocking collectives: 14.9 us -> 13.1 us
    ppermute x15, waiting for transfers between devices: 28 us -> 13.1 us  [body(): got0.append(send if dz == dc == 0 else lax.ppermute(send, 'member', pairs))]
    ppermute x15, starting transfers between devices: 26.7 us -> 38.1 us  [body(): got0.append(send if dz == dc == 0 else lax.ppermute(send, 'member', pairs))]
    all_to_all x1, blocking collectives: 14.9 us -> 13.1 us  [body(): arrived = lax.all_to_all(packed, 'member', 0, 0, tiled=True)]
  transfers between devices with their start and end apart: 16 -> 16, of which waited for: 6 -> 4; matrix products, arithmetic and copies ran while one was open for 0% -> 0% of each run, Pallas kernels for 20% -> 21%
where the time goes in v3:
time: 112 us
  starting transfers between devices  48.1 us (43%)
  Pallas kernels  36.7 us (33%)
  waiting for transfers between devices  13.1 us (12%)
  blocking collectives  13.1 us (12%)
    ppermute x15, starting transfers between devices, body(): got0.append(send if dz == dc == 0 else lax.ppermute(send, 'member', pairs))  38.1 us
    pallas_call x1, Pallas kernels, body(): call(first_kernel, pltpu.HBM((CHUNKS[0], LAT), F32), [HB] * GROUPS + [HB,...  15.9 us
    all_to_all x1, blocking collectives, body(): arrived = lax.all_to_all(packed, 'member', 0, 0, tiled=True)  13.1 us
    ppermute x15, waiting for transfers between devices, body(): got0.append(send if dz == dc == 0 else lax.ppermute(send, 'member', pairs))  13.1 us
    all_to_all x1, starting transfers between devices, body(): got1 = lax.all_to_all(send1, 'member', 0, 0, tiled=True)  9.98 us
    pallas_call x1, Pallas kernels, body(): call(last_kernel, shape((GROUPS, 16, 128), F32), [VM] + [HB] * 5, VM, ext...  8.97 us
    pallas_call x1, Pallas kernels, body(): call(early_kernel, [(shape if any(o) else pltpu.HBM)((LOCAL * CHUNKS[0],...  4.04 us
    pallas_call x1, Pallas kernels, body(): call(late_kernel, [shape((GROUPS, LOCAL * CHUNKS[1], LAT), BF16), shape((...  3.78 us
  transfers between devices with their start and end apart: 16, of which 4 were waited for; matrix products, arithmetic and copies ran while one was open for 0% of the time, Pallas kernels for 21%

profile of v3, /device:TPU:1, one launch (start us, length us, event | category | flops | bytes accessed | tf_op | source)
XLA Modules:
  0.0 111.8 jit_solution(12246245684492401128)
XLA Ops:
  0.0 3.8 %shard_map.91 = (bf16[16,48,512]{2,1,0:T(8,128)(2,1)}, bf16[768,768]{1,0:T(8,128)(2,1)S(1)}) custom-call(s32[768]{0:T(1024)} %order.3, s32[3]{0:T(128)} %seeds.3, bf16[768,512]{1,0:T(8,128)(2,1)} %latents.3, bf16[3,768,512]{2,1,0:T(8,128)(2,1)} %perturbation.3, f32[64,512]{1,0:T(8,128)} %table.3), custom_call_target="tpu_custom_call" | custom-call | flops 1000000000 | tf_op jit(solution)/shard_map/pallas_call | solution.py:320
  3.8 10.0 %all-to-all-start = ((bf16[16,48,512]{2,1,0:T(8,128)(2,1)}), bf16[16,48,512]{2,1,0:T(8,128)(2,1)S(1)}, u32[]{:S(2)}, u32[]{:S(2)}) async-start(bf16[16,48,512]{2,1,0:T(8,128)(2,1)} %get-tuple-element.27), calls=%async_computation | async-start | bytes 1572864 | tf_op jit(solution)/shard_map/all_to_all | solution.py:329
  13.8 4.0 %shard_map.93 = (bf16[96,512]{1,0:T(8,128)(2,1)S(1)}, bf16[96,512]{1,0:T(8,128)(2,1)S(1)}, bf16[96,512]{1,0:T(8,128)(2,1)S(1)}, bf16[96,512]{1,0:T(8,128)(2,1)S(...) custom-call(s32[1]{0:T(128)} %bitcast.1.me, ...), custom_call_target="tpu_custom_call" | custom-call | tf_op jit(solution)/shard_map/pallas_call | solution.py:308
  17.8 3.2 %collective-permute-start = (bf16[96,512]{1,0:T(8,128)(2,1)S(1)}, bf16[96,512]{1,0:T(8,128)(2,1)S(1)}, u32[]{:S(2)}, u32[]{:S(2)}) collective-permute-start(bf16[96,512]{1,0:T(8,128)(2,1)S(1)} %get-tuple-element.30), channel_id=1, source_target_pairs={{0,96},{16,112},{32,128},{48,144},{64,160},{80,176},{96,192},{112,... | collective-permute-start | bytes 294920 | tf_op jit(solution)/shard_map/ppermute | solution.py:319
  21.0 3.0 %collective-permute-start.1 = (bf16[96,512]{1,0:T(8,128)(2,1)S(1)}, bf16[96,512]{1,0:T(8,128)(2,1)S(1)}, u32[]{:S(2)}, u32[]{:S(2)}) collective-permute-start(bf16[96,512]{1,0:T(8,128)(2,1)S(1)} %get-tuple-element.31), channel_id=1, source_target_pairs={{0,112},{16,96},{32,144},{48,128},{64,176},{80,160},{96,208},{112,... | collective-permute-start | bytes 294920 | tf_op jit(solution)/shard_map/ppermute | solution.py:319
  24.0 2.1 %collective-permute-start.2 = (bf16[96,512]{1,0:T(8,128)(2,1)S(1)}, bf16[96,512]{1,0:T(8,128)(2,1)S(1)}, u32[]{:S(2)}, u32[]{:S(2)}) collective-permute-start(bf16[96,512]{1,0:T(8,128)(2,1)S(1)} %get-tuple-element.32), channel_id=1, source_target_pairs={{0,160},{16,176},{32,192},{48,208},{64,224},{80,240},{96,0},{112,1... | collective-permute-start | bytes 294920 | tf_op jit(solution)/shard_map/ppermute | solution.py:319
  26.1 1.5 %collective-permute-start.3 = (bf16[96,512]{1,0:T(8,128)(2,1)S(1)}, bf16[96,512]{1,0:T(8,128)(2,1)S(1)}, u32[]{:S(2)}, u32[]{:S(2)}) collective-permute-start(bf16[96,512]{1,0:T(8,128)(2,1)S(1)} %get-tuple-element.33), channel_id=1, source_target_pairs={{0,176},{16,160},{32,208},{48,192},{64,240},{80,224},{96,16},{112,... | collective-permute-start | bytes 294920 | tf_op jit(solution)/shard_map/ppermute | solution.py:319
  27.6 5.1 %collective-permute-start.4 = (bf16[96,512]{1,0:T(8,128)(2,1)S(1)}, bf16[96,512]{1,0:T(8,128)(2,1)S(1)}, u32[]{:S(2)}, u32[]{:S(2)}) collective-permute-start(bf16[96,512]{1,0:T(8,128)(2,1)S(1)} %get-tuple-element.34), channel_id=1, source_target_pairs={{0,128},{16,144},{32,160},{48,176},{64,192},{80,208},{96,224},{112... | collective-permute-start | bytes 294920 | tf_op jit(solution)/shard_map/ppermute | solution.py:319
  32.7 8.4 %collective-permute-done.refs_0_ = bf16[96,512]{1,0:T(8,128)(2,1)S(1)} collective-permute-done((bf16[96,512]{1,0:T(8,128)(2,1)S(1)}, bf16[96,512]{1,0:T(8,128)(2,1)S(1)}, u32[]{:S(2)}, u32[]{:S(2)}) %collective-permute-start) | collective-permute-done | bytes 98336 | tf_op jit(solution)/shard_map/ppermute | solution.py:319
  41.0 3.2 %collective-permute-start.5 = (bf16[96,512]{1,0:T(8,128)(2,1)S(1)}, bf16[96,512]{1,0:T(8,128)(2,1)S(1)}, u32[]{:S(2)}, u32[]{:S(2)}) collective-permute-start(bf16[96,512]{1,0:T(8,128)(2,1)S(1)} %get-tuple-element.35), channel_id=1, source_target_pairs={{0,144},{16,128},{32,176},{48,160},{64,208},{80,192},{96,240},{112... | collective-permute-start | bytes 294920 | tf_op jit(solution)/shard_map/ppermute | solution.py:319
  44.3 4.2 %collective-permute-done.1.refs_1_ = bf16[96,512]{1,0:T(8,128)(2,1)S(1)} collective-permute-done((bf16[96,512]{1,0:T(8,128)(2,1)S(1)}, bf16[96,512]{1,0:T(8,128)(2,1)S(1)}, u32[]{:S(2)}, u32[]{:S(2)}) %collective-permute-start.1) | collective-permute-done | bytes 98336 | tf_op jit(solution)/shard_map/ppermute | solution.py:319
  48.4 0.0 collective-permute-start.6
  48.4 0.0 collective-permute-done.2.refs_2_
  48.5 3.1 %collective-permute-start.7 = (bf16[96,512]{1,0:T(8,128)(2,1)S(1)}, bf16[96,512]{1,0:T(8,128)(2,1)S(1)}, u32[]{:S(2)}, u32[]{:S(2)}) collective-permute-start(bf16[96,512]{1,0:T(8,128)(2,1)S(1)} %get-tuple-element.37), channel_id=1, source_target_pairs={{0,80},{16,64},{32,112},{48,96},{64,144},{80,128},{96,176},{112,16... | collective-permute-start | bytes 294920 | tf_op jit(solution)/shard_map/ppermute | solution.py:319
  51.6 0.5 collective-permute-start.8
  52.1 0.1 collective-permute-done.4.refs_4_
  52.2 4.6 %collective-permute-start.9 = (bf16[96,512]{1,0:T(8,128)(2,1)S(1)}, bf16[96,512]{1,0:T(8,128)(2,1)S(1)}, u32[]{:S(2)}, u32[]{:S(2)}) collective-permute-start(bf16[96,512]{1,0:T(8,128)(2,1)S(1)} %get-tuple-element.39), channel_id=1, source_target_pairs={{0,208},{16,192},{32,240},{48,224},{64,16},{80,0},{96,48},{112,32}... | collective-permute-start | bytes 294920 | tf_op jit(solution)/shard_map/ppermute | solution.py:319
  56.8 2.1 %collective-permute-start.10 = (bf16[96,512]{1,0:T(8,128)(2,1)S(1)}, bf16[96,512]{1,0:T(8,128)(2,1)S(1)}, u32[]{:S(2)}, u32[]{:S(2)}) collective-permute-start(bf16[96,512]{1,0:T(8,128)(2,1)S(1)} %get-tuple-element.40), channel_id=1, source_target_pairs={{0,32},{16,48},{32,64},{48,80},{64,96},{80,112},{96,128},{112,144}... | collective-permute-start | bytes 294920 | tf_op jit(solution)/shard_map/ppermute | solution.py:319
  58.9 5.6 %collective-permute-start.11 = (bf16[96,512]{1,0:T(8,128)(2,1)S(1)}, bf16[96,512]{1,0:T(8,128)(2,1)S(1)}, u32[]{:S(2)}, u32[]{:S(2)}) collective-permute-start(bf16[96,512]{1,0:T(8,128)(2,1)S(1)} %get-tuple-element.41), channel_id=1, source_target_pairs={{0,48},{16,32},{32,80},{48,64},{64,112},{80,96},{96,144},{112,128}... | collective-permute-start | bytes 294920 | tf_op jit(solution)/shard_map/ppermute | solution.py:319
  64.5 2.3 %collective-permute-start.12 = (bf16[96,512]{1,0:T(8,128)(2,1)S(1)}, bf16[96,512]{1,0:T(8,128)(2,1)S(1)}, u32[]{:S(2)}, u32[]{:S(2)}) collective-permute-start(bf16[96,512]{1,0:T(8,128)(2,1)S(1)} %get-tuple-element.42), channel_id=1, source_target_pairs={{0,224},{16,240},{32,0},{48,16},{64,32},{80,48},{96,64},{112,80},{... | collective-permute-start | bytes 294920 | tf_op jit(solution)/shard_map/ppermute | solution.py:319
  66.8 1.8 %collective-permute-start.13 = (bf16[96,512]{1,0:T(8,128)(2,1)S(1)}, bf16[96,512]{1,0:T(8,128)(2,1)S(1)}, u32[]{:S(2)}, u32[]{:S(2)}) collective-permute-start(bf16[96,512]{1,0:T(8,128)(2,1)S(1)} %get-tuple-element.43), channel_id=1, source_target_pairs={{0,240},{16,224},{32,16},{48,0},{64,48},{80,32},{96,80},{112,64},{... | collective-permute-start | bytes 294920 | tf_op jit(solution)/shard_map/ppermute | solution.py:319
  68.6 3.0 %shard_map.92 = (f32[48,384]{1,0:T(8,128)}, bf16[512,1024]{1,0:T(8,128)(2,1)S(1)}, bf16[512,1024]{1,0:T(8,128)(2,1)S(1)}, bf16[1024,384]{1,0:T(8,128)(2,1)S(1)}) custom-call(s32[1]{0:T(128)} %bitcast.1.me, bf16[768,768]{1,0:T(8,128)(2,1)S(1)} %get-tuple-element.28.pick, bf16[768,384]{1,0:T(8,128)(2,1)} %targets.1, bf16[512,1024]{1,0:T(8,128)(2,1)} %w_gate.3, ...), custom_call_target="tpu_custom_call" | custom-call | flops 10000000 | tf_op jit(solution)/shard_map/pallas_call | solution.py:331
  71.7 0.5 collective-permute-done.13.refs_13_
  72.2 0.0 copy-done.10
  72.2 0.0 copy-done.11
  72.3 0.0 copy-done.12
  72.3 0.4 copy-done.13
  72.8 0.0 copy-done.14
  72.8 15.9 %shard_map.94.earlier = f32[32,512]{1,0:T(8,128)} custom-call(bf16[96,512]{1,0:T(8,128)(2,1)} %copy-done, bf16[96,512]{1,0:T(8,128)(2,1)} %copy-done.1, bf16[96,512]{1,0:T(8,128)(2,1)} %copy-done.2, bf16[96,512]{1,0:T(8,128)(2,1)} %copy-done.3, bf16[96,512]{1,0:T(8,128)(2,1)} %copy-done.4, bf16[96,512]{1,0:T(8,128)(2,1)} %copy-done.5, ...), custom_call_target="tpu_custom_call" | custom-call | flops 10000000000 | tf_op jit(solution)/shard_map/pallas_call | solution.py:340
  88.7 9.0 %shard_map.95 = f32[16,16,128]{2,1,0:T(8,128)S(1)} custom-call(bf16[768,512]{1,0:T(8,128)(2,1)S(1)} %bitcast.3, f32[48,384]{1,0:T(8,128)} %get-tuple-element.29.refs_16_.target, bf16[512,1024]{1,0:T(8,128)(2,1)} %w_gate.3, bf16[512,1024]{1,0:T(8,128)(2,1)} %w_up.3, bf16[1024,384]{1,0:T(8,128)(2,1)} %lowering.3, f32[32,512]{1,0:T(8,128)} %shard_map.94.earlier), custom_call_target="tpu_custom_call" | custom-call | flops 5000000000 | tf_op jit(solution)/shard_map/pallas_call | solution.py:356
  97.7 13.1 %all_to_all.10.arrived = f32[16,16,128]{2,1,0:T(8,128)S(1)} all-to-all(f32[16,16,128]{2,1,0:T(8,128)S(1)} %shard_map.95), channel_id=1, replica_groups=mesh['member'=16,'space'=16] {'member'}, dimensions={0} | all-to-all | bytes 262144 | tf_op jit(solution)/shard_map/all_to_all | solution.py:359
  110.8 1.0 shard_map.96
  (37 shorter events, 0.1 us)
Async XLA Ops:
  3.8 84.9 %all-to-all-start = ((bf16[16,48,512]{2,1,0:T(8,128)(2,1)}), bf16[16,48,512]{2,1,0:T(8,128)(2,1)S(1)}, u32[]{:S(2)}, u32[]{:S(2)}) async-start(bf16[16,48,512]{2,1,0:T(8,128)(2,1)} %get-tuple-element.27), calls=%async_computation | async-start | bytes 1572864 | tf_op jit(solution)/shard_map/all_to_all | solution.py:329
  17.8 23.2 %collective-permute-start = (bf16[96,512]{1,0:T(8,128)(2,1)S(1)}, bf16[96,512]{1,0:T(8,128)(2,1)S(1)}, u32[]{:S(2)}, u32[]{:S(2)}) collective-permute-start(bf16[96,512]{1,0:T(8,128)(2,1)S(1)} %get-tuple-element.30), channel_id=1, source_target_pairs={{0,96},{16,112},{32,128},{48,144},{64,160},{80,176},{96,192},{112,... | collective-permute-start | bytes 294920 | tf_op jit(solution)/shard_map/ppermute | solution.py:319
  21.0 27.4 %collective-permute-start.1 = (bf16[96,512]{1,0:T(8,128)(2,1)S(1)}, bf16[96,512]{1,0:T(8,128)(2,1)S(1)}, u32[]{:S(2)}, u32[]{:S(2)}) collective-permute-start(bf16[96,512]{1,0:T(8,128)(2,1)S(1)} %get-tuple-element.31), channel_id=1, source_target_pairs={{0,112},{16,96},{32,144},{48,128},{64,176},{80,160},{96,208},{112,... | collective-permute-start | bytes 294920 | tf_op jit(solution)/shard_map/ppermute | solution.py:319
  24.0 24.4 %collective-permute-start.2 = (bf16[96,512]{1,0:T(8,128)(2,1)S(1)}, bf16[96,512]{1,0:T(8,128)(2,1)S(1)}, u32[]{:S(2)}, u32[]{:S(2)}) collective-permute-start(bf16[96,512]{1,0:T(8,128)(2,1)S(1)} %get-tuple-element.32), channel_id=1, source_target_pairs={{0,160},{16,176},{32,192},{48,208},{64,224},{80,240},{96,0},{112,1... | collective-permute-start | bytes 294920 | tf_op jit(solution)/shard_map/ppermute | solution.py:319
  26.1 25.5 %collective-permute-start.3 = (bf16[96,512]{1,0:T(8,128)(2,1)S(1)}, bf16[96,512]{1,0:T(8,128)(2,1)S(1)}, u32[]{:S(2)}, u32[]{:S(2)}) collective-permute-start(bf16[96,512]{1,0:T(8,128)(2,1)S(1)} %get-tuple-element.33), channel_id=1, source_target_pairs={{0,176},{16,160},{32,208},{48,192},{64,240},{80,224},{96,16},{112,... | collective-permute-start | bytes 294920 | tf_op jit(solution)/shard_map/ppermute | solution.py:319
  27.6 24.6 %collective-permute-start.4 = (bf16[96,512]{1,0:T(8,128)(2,1)S(1)}, bf16[96,512]{1,0:T(8,128)(2,1)S(1)}, u32[]{:S(2)}, u32[]{:S(2)}) collective-permute-start(bf16[96,512]{1,0:T(8,128)(2,1)S(1)} %get-tuple-element.34), channel_id=1, source_target_pairs={{0,128},{16,144},{32,160},{48,176},{64,192},{80,208},{96,224},{112... | collective-permute-start | bytes 294920 | tf_op jit(solution)/shard_map/ppermute | solution.py:319
  41.0 31.1 %copy-start = (bf16[96,512]{1,0:T(8,128)(2,1)}, bf16[96,512]{1,0:T(8,128)(2,1)S(1)}, u32[]{:S(2)}) copy-start(bf16[96,512]{1,0:T(8,128)(2,1)S(1)} %collective-permute-done.refs_0_) | copy-start | bytes 294916
  41.0 15.8 %collective-permute-start.5 = (bf16[96,512]{1,0:T(8,128)(2,1)S(1)}, bf16[96,512]{1,0:T(8,128)(2,1)S(1)}, u32[]{:S(2)}, u32[]{:S(2)}) collective-permute-start(bf16[96,512]{1,0:T(8,128)(2,1)S(1)} %get-tuple-element.35), channel_id=1, source_target_pairs={{0,144},{16,128},{32,176},{48,160},{64,208},{80,192},{96,240},{112... | collective-permute-start | bytes 294920 | tf_op jit(solution)/shard_map/ppermute | solution.py:319
  48.4 23.7 %copy-start.1 = (bf16[96,512]{1,0:T(8,128)(2,1)}, bf16[96,512]{1,0:T(8,128)(2,1)S(1)}, u32[]{:S(2)}) copy-start(bf16[96,512]{1,0:T(8,128)(2,1)S(1)} %collective-permute-done.1.refs_1_) | copy-start | bytes 294916
  48.4 10.5 %collective-permute-start.6 = (bf16[96,512]{1,0:T(8,128)(2,1)S(1)}, bf16[96,512]{1,0:T(8,128)(2,1)S(1)}, u32[]{:S(2)}, u32[]{:S(2)}) collective-permute-start(bf16[96,512]{1,0:T(8,128)(2,1)S(1)} %get-tuple-element.36), channel_id=1, source_target_pairs={{0,64},{16,80},{32,96},{48,112},{64,128},{80,144},{96,160},{112,17... | collective-permute-start | bytes 294920 | tf_op jit(solution)/shard_map/ppermute | solution.py:319
  48.5 23.7 %copy-start.2 = (bf16[96,512]{1,0:T(8,128)(2,1)}, bf16[96,512]{1,0:T(8,128)(2,1)S(1)}, u32[]{:S(2)}) copy-start(bf16[96,512]{1,0:T(8,128)(2,1)S(1)} %collective-permute-done.2.refs_2_) | copy-start | bytes 294916
  48.5 16.0 %collective-permute-start.7 = (bf16[96,512]{1,0:T(8,128)(2,1)S(1)}, bf16[96,512]{1,0:T(8,128)(2,1)S(1)}, u32[]{:S(2)}, u32[]{:S(2)}) collective-permute-start(bf16[96,512]{1,0:T(8,128)(2,1)S(1)} %get-tuple-element.37), channel_id=1, source_target_pairs={{0,80},{16,64},{32,112},{48,96},{64,144},{80,128},{96,176},{112,16... | collective-permute-start | bytes 294920 | tf_op jit(solution)/shard_map/ppermute | solution.py:319
  51.6 20.6 %copy-start.3 = (bf16[96,512]{1,0:T(8,128)(2,1)}, bf16[96,512]{1,0:T(8,128)(2,1)S(1)}, u32[]{:S(2)}) copy-start(bf16[96,512]{1,0:T(8,128)(2,1)S(1)} %collective-permute-done.3.refs_3_) | copy-start | bytes 294916
  51.6 15.2 %collective-permute-start.8 = (bf16[96,512]{1,0:T(8,128)(2,1)S(1)}, bf16[96,512]{1,0:T(8,128)(2,1)S(1)}, u32[]{:S(2)}, u32[]{:S(2)}) collective-permute-start(bf16[96,512]{1,0:T(8,128)(2,1)S(1)} %get-tuple-element.38), channel_id=1, source_target_pairs={{0,192},{16,208},{32,224},{48,240},{64,0},{80,16},{96,32},{112,48}... | collective-permute-start | bytes 294920 | tf_op jit(solution)/shard_map/ppermute | solution.py:319
  52.2 20.0 %copy-start.4 = (bf16[96,512]{1,0:T(8,128)(2,1)}, bf16[96,512]{1,0:T(8,128)(2,1)S(1)}, u32[]{:S(2)}) copy-start(bf16[96,512]{1,0:T(8,128)(2,1)S(1)} %collective-permute-done.4.refs_4_) | copy-start | bytes 294916
  52.2 16.4 %collective-permute-start.9 = (bf16[96,512]{1,0:T(8,128)(2,1)S(1)}, bf16[96,512]{1,0:T(8,128)(2,1)S(1)}, u32[]{:S(2)}, u32[]{:S(2)}) collective-permute-start(bf16[96,512]{1,0:T(8,128)(2,1)S(1)} %get-tuple-element.39), channel_id=1, source_target_pairs={{0,208},{16,192},{32,240},{48,224},{64,16},{80,0},{96,48},{112,32}... | collective-permute-start | bytes 294920 | tf_op jit(solution)/shard_map/ppermute | solution.py:319
  56.8 15.3 %copy-start.5 = (bf16[96,512]{1,0:T(8,128)(2,1)}, bf16[96,512]{1,0:T(8,128)(2,1)S(1)}, u32[]{:S(2)}) copy-start(bf16[96,512]{1,0:T(8,128)(2,1)S(1)} %collective-permute-done.5.refs_5_) | copy-start | bytes 294916
  56.8 14.8 %collective-permute-start.10 = (bf16[96,512]{1,0:T(8,128)(2,1)S(1)}, bf16[96,512]{1,0:T(8,128)(2,1)S(1)}, u32[]{:S(2)}, u32[]{:S(2)}) collective-permute-start(bf16[96,512]{1,0:T(8,128)(2,1)S(1)} %get-tuple-element.40), channel_id=1, source_target_pairs={{0,32},{16,48},{32,64},{48,80},{64,96},{80,112},{96,128},{112,144}... | collective-permute-start | bytes 294920 | tf_op jit(solution)/shard_map/ppermute | solution.py:319
  58.9 13.3 %copy-start.6 = (bf16[96,512]{1,0:T(8,128)(2,1)}, bf16[96,512]{1,0:T(8,128)(2,1)S(1)}, u32[]{:S(2)}) copy-start(bf16[96,512]{1,0:T(8,128)(2,1)S(1)} %collective-permute-done.6.refs_6_) | copy-start | bytes 294916
  58.9 12.7 %collective-permute-start.11 = (bf16[96,512]{1,0:T(8,128)(2,1)S(1)}, bf16[96,512]{1,0:T(8,128)(2,1)S(1)}, u32[]{:S(2)}, u32[]{:S(2)}) collective-permute-start(bf16[96,512]{1,0:T(8,128)(2,1)S(1)} %get-tuple-element.41), channel_id=1, source_target_pairs={{0,48},{16,32},{32,80},{48,64},{64,112},{80,96},{96,144},{112,128}... | collective-permute-start | bytes 294920 | tf_op jit(solution)/shard_map/ppermute | solution.py:319
  64.5 7.7 %copy-start.7 = (bf16[96,512]{1,0:T(8,128)(2,1)}, bf16[96,512]{1,0:T(8,128)(2,1)S(1)}, u32[]{:S(2)}) copy-start(bf16[96,512]{1,0:T(8,128)(2,1)S(1)} %collective-permute-done.7.refs_7_) | copy-start | bytes 294916
  64.5 7.1 %collective-permute-start.12 = (bf16[96,512]{1,0:T(8,128)(2,1)S(1)}, bf16[96,512]{1,0:T(8,128)(2,1)S(1)}, u32[]{:S(2)}, u32[]{:S(2)}) collective-permute-start(bf16[96,512]{1,0:T(8,128)(2,1)S(1)} %get-tuple-element.42), channel_id=1, source_target_pairs={{0,224},{16,240},{32,0},{48,16},{64,32},{80,48},{96,64},{112,80},{... | collective-permute-start | bytes 294920 | tf_op jit(solution)/shard_map/ppermute | solution.py:319
  66.8 5.4 %copy-start.8 = (bf16[96,512]{1,0:T(8,128)(2,1)}, bf16[96,512]{1,0:T(8,128)(2,1)S(1)}, u32[]{:S(2)}) copy-start(bf16[96,512]{1,0:T(8,128)(2,1)S(1)} %collective-permute-done.8.refs_8_) | copy-start | bytes 294916
  66.8 5.3 %collective-permute-start.13 = (bf16[96,512]{1,0:T(8,128)(2,1)S(1)}, bf16[96,512]{1,0:T(8,128)(2,1)S(1)}, u32[]{:S(2)}, u32[]{:S(2)}) collective-permute-start(bf16[96,512]{1,0:T(8,128)(2,1)S(1)} %get-tuple-element.43), channel_id=1, source_target_pairs={{0,240},{16,224},{32,16},{48,0},{64,48},{80,32},{96,80},{112,64},{... | collective-permute-start | bytes 294920 | tf_op jit(solution)/shard_map/ppermute | solution.py:319
  68.6 3.7 %copy-start.9 = (bf16[96,512]{1,0:T(8,128)(2,1)}, bf16[96,512]{1,0:T(8,128)(2,1)S(1)}, u32[]{:S(2)}) copy-start(bf16[96,512]{1,0:T(8,128)(2,1)S(1)} %collective-permute-done.9.refs_9_) | copy-start | bytes 294916
  68.6 3.6 %collective-permute-start.14 = (bf16[96,512]{1,0:T(8,128)(2,1)S(1)}, bf16[96,512]{1,0:T(8,128)(2,1)S(1)}, u32[]{:S(2)}, u32[]{:S(2)}) collective-permute-start(bf16[96,512]{1,0:T(8,128)(2,1)S(1)} %get-tuple-element.45), channel_id=1, source_target_pairs={{0,16},{16,0},{32,48},{48,32},{64,80},{80,64},{96,112},{112,96},{1... | collective-permute-start | bytes 294920 | tf_op jit(solution)/shard_map/ppermute | solution.py:319
  71.6 0.6 copy-start.10
  71.6 0.7 copy-start.11
  71.6 0.7 copy-start.12
  72.1 0.6 copy-start.13
  72.1 0.7 copy-start.14

commit v4 on v3

--- a/solution.py
+++ b/solution.py
@@ -17,7 +17,10 @@
 LOCAL = 3
 MEMBERS = 48
 Z = 8
-OFFSETS = tuple((dz, dc) for dz in (3, 5, 4, 2, 6, 1, 7, 0) for dc in (0, 1))
+OFFSETS = (
+    *((1, 0), (7, 0), (3, 0), (5, 0), (4, 0), (4, 1), (3, 1), (5, 1)),
+    *((2, 0), (6, 0), (2, 1), (6, 1), (1, 1), (7, 1), (0, 1), (0, 0)),
+)
 CHUNKS = (32, 16)
 STARTS = (0, 32)
 SCALE = float(PIECE * OUT) ** 0.5
@@ -158,7 +161,7 @@
             cotangent[j, at, :] = made[:, 128 * j : 128 * j + 128]
 
 
-def network(noisy, target, w_gate, w_up, lowering, state, count, start):
+def network(noisy, target, w_gate, w_up, lowering, state, count, start, pending=()):
     left, right, forecast, cotangent, gate_sum, up_sum, target_here, sem = state[:8]
     copy = pltpu.make_async_copy(target.at[pl.ds(start, count)], target_here, sem)
     copy.start()
@@ -167,22 +170,35 @@
     inside = block // count
     gap_rows = count + PAD
 
-    @pl.loop(0, total // block)
-    def _(i):
-        at = pl.ds(pl.multiple_of(i * block, block), block)
+    def forward(i, pending=()):
+        known = isinstance(i, int)
+        at = pl.ds(i * block if known else pl.multiple_of(i * block, block), block)
         x = noisy[at, :]
+        for late in pending[:1]:
+            late.wait()
         half = 0.5 * dot(x, w_gate[...])
+        for late in pending[1:2]:
+            late.wait()
         up = dot(x, w_up[...])
         bent = 1.0 + jnp.tanh(half)
         swish = half * bent
         s = 0.5 * bent
         right[at, :] = swish
         left[at, :] = up * (s + swish * (1.0 - s))
+        for late in pending[2:]:
+            late.wait()
         made = dot((swish * up).astype(BF16), lowering[...]).astype(BF16).astype(F32)
         for q in range(inside):
-            to = pl.ds(pl.multiple_of(i * inside * gap_rows + q * gap_rows, 8), count)
+            to = i * inside * gap_rows + q * gap_rows
+            to = pl.ds(to if known else pl.multiple_of(to, 8), count)
             for j in range(3):
                 forecast[j, to, :] = made[count * q : count * q + count, 128 * j : 128 * j + 128]
+
+    if pending:
+        for i in range(total // block):
+            forward(i, () if i else pending)
+    else:
+        pl.loop(0, total // block)(forward)
 
     copy.wait()
 
@@ -240,9 +256,10 @@
     ]
     for copy in copies:
         copy.start()
-    for copy in copies:
-        copy.wait()
-    grad = network(noisy, target, gate_here, up_here, low_here, state, CHUNKS[1], STARTS[1])
+    grad = network(
+        noisy, target, gate_here, up_here, low_here, state, CHUNKS[1], STARTS[1], (copies[0], copies[1], copies[2])
+    )
+    copies[3].wait()
     parts = (here[:16], here[16:], grad)
     blank = jnp.zeros((16, 32), F32)
     for d in range(GROUPS):

time: 112 us -> 109 us (0.973)
  starting transfers between devices: 48.1 us -> 45 us
    ppermute x15, starting transfers between devices: 38.1 us -> 35 us  [body(): got0.append(send if dz == dc == 0 else lax.ppermute(send, 'member', pairs))]
  transfers between devices with their start and end apart: 16 -> 16, of which waited for: 4 -> 5; matrix products, arithmetic and copies ran while one was open for 0% -> 0% of each run, Pallas kernels for 21% -> 21%
where the time goes in v4:
time: 109 us
  starting transfers between devices  45 us (41%)
  Pallas kernels  36.4 us (33%)
  waiting for transfers between devices  14.1 us (13%)
  blocking collectives  12.8 us (12%)
    ppermute x15, starting transfers between devices, body(): got0.append(send if dz == dc == 0 else lax.ppermute(send, 'member', pairs))  35 us
    pallas_call x1, Pallas kernels, body(): call(first_kernel, pltpu.HBM((CHUNKS[0], LAT), F32), [HB] * GROUPS + [HB,...  15.9 us
    ppermute x15, waiting for transfers between devices, body(): got0.append(send if dz == dc == 0 else lax.ppermute(send, 'member', pairs))  14.1 us
    all_to_all x1, blocking collectives, body(): arrived = lax.all_to_all(packed, 'member', 0, 0, tiled=True)  12.8 us
    all_to_all x1, starting transfers between devices, body(): got1 = lax.all_to_all(send1, 'member', 0, 0, tiled=True)  9.98 us
    pallas_call x1, Pallas kernels, body(): call(last_kernel, shape((GROUPS, 16, 128), F32), [VM] + [HB] * 5, VM, ext...  8.67 us
    pallas_call x1, Pallas kernels, body(): call(early_kernel, [(shape if any(o) else pltpu.HBM)((LOCAL * CHUNKS[0],...  4.05 us
    pallas_call x1, Pallas kernels, body(): call(late_kernel, [shape((GROUPS, LOCAL * CHUNKS[1], LAT), BF16), shape((...  3.78 us
  transfers between devices with their start and end apart: 16, of which 5 were waited for; matrix products, arithmetic and copies ran while one was open for 0% of the time, Pallas kernels for 21%

profile of v4, /device:TPU:1, one launch (start us, length us, event | category | flops | bytes accessed | tf_op | source)
XLA Modules:
  0.0 109.0 jit_solution(2844918957103408531)
XLA Ops:
  0.0 3.8 %shard_map.91 = (bf16[16,48,512]{2,1,0:T(8,128)(2,1)}, bf16[768,768]{1,0:T(8,128)(2,1)S(1)}) custom-call(s32[768]{0:T(1024)} %order.3, s32[3]{0:T(128)} %seeds.3, bf16[768,512]{1,0:T(8,128)(2,1)} %latents.3, bf16[3,768,512]{2,1,0:T(8,128)(2,1)} %perturbation.3, f32[64,512]{1,0:T(8,128)} %table.3), custom_call_target="tpu_custom_call" | custom-call | flops 1000000000 | tf_op jit(solution)/shard_map/pallas_call | solution.py:337
  3.8 10.0 %all-to-all-start = ((bf16[16,48,512]{2,1,0:T(8,128)(2,1)}), bf16[16,48,512]{2,1,0:T(8,128)(2,1)S(1)}, u32[]{:S(2)}, u32[]{:S(2)}) async-start(bf16[16,48,512]{2,1,0:T(8,128)(2,1)} %get-tuple-element.27), calls=%async_computation | async-start | bytes 1572864 | tf_op jit(solution)/shard_map/all_to_all | solution.py:346
  13.8 4.0 %shard_map.93 = (bf16[96,512]{1,0:T(8,128)(2,1)S(1)}, bf16[96,512]{1,0:T(8,128)(2,1)S(1)}, bf16[96,512]{1,0:T(8,128)(2,1)S(1)}, bf16[96,512]{1,0:T(8,128)(2,1)S(...) custom-call(s32[1]{0:T(128)} %bitcast.1.me, ...), custom_call_target="tpu_custom_call" | custom-call | tf_op jit(solution)/shard_map/pallas_call | solution.py:325
  17.8 1.4 %collective-permute-start = (bf16[96,512]{1,0:T(8,128)(2,1)S(1)}, bf16[96,512]{1,0:T(8,128)(2,1)S(1)}, u32[]{:S(2)}, u32[]{:S(2)}) collective-permute-start(bf16[96,512]{1,0:T(8,128)(2,1)S(1)} %get-tuple-element.30), channel_id=1, source_target_pairs={{0,32},{16,48},{32,64},{48,80},{64,96},{80,112},{96,128},{112,144}... | collective-permute-start | bytes 294920 | tf_op jit(solution)/shard_map/ppermute | solution.py:336
  19.3 1.3 %collective-permute-start.1 = (bf16[96,512]{1,0:T(8,128)(2,1)S(1)}, bf16[96,512]{1,0:T(8,128)(2,1)S(1)}, u32[]{:S(2)}, u32[]{:S(2)}) collective-permute-start(bf16[96,512]{1,0:T(8,128)(2,1)S(1)} %get-tuple-element.31), channel_id=1, source_target_pairs={{0,224},{16,240},{32,0},{48,16},{64,32},{80,48},{96,64},{112,80},{... | collective-permute-start | bytes 294920 | tf_op jit(solution)/shard_map/ppermute | solution.py:336
  20.6 2.9 %collective-permute-start.2 = (bf16[96,512]{1,0:T(8,128)(2,1)S(1)}, bf16[96,512]{1,0:T(8,128)(2,1)S(1)}, u32[]{:S(2)}, u32[]{:S(2)}) collective-permute-start(bf16[96,512]{1,0:T(8,128)(2,1)S(1)} %get-tuple-element.32), channel_id=1, source_target_pairs={{0,96},{16,112},{32,128},{48,144},{64,160},{80,176},{96,192},{112,... | collective-permute-start | bytes 294920 | tf_op jit(solution)/shard_map/ppermute | solution.py:336
  23.5 1.6 %collective-permute-start.3 = (bf16[96,512]{1,0:T(8,128)(2,1)S(1)}, bf16[96,512]{1,0:T(8,128)(2,1)S(1)}, u32[]{:S(2)}, u32[]{:S(2)}) collective-permute-start(bf16[96,512]{1,0:T(8,128)(2,1)S(1)} %get-tuple-element.33), channel_id=1, source_target_pairs={{0,160},{16,176},{32,192},{48,208},{64,224},{80,240},{96,0},{112,1... | collective-permute-start | bytes 294920 | tf_op jit(solution)/shard_map/ppermute | solution.py:336
  25.1 5.3 %collective-permute-start.4 = (bf16[96,512]{1,0:T(8,128)(2,1)S(1)}, bf16[96,512]{1,0:T(8,128)(2,1)S(1)}, u32[]{:S(2)}, u32[]{:S(2)}) collective-permute-start(bf16[96,512]{1,0:T(8,128)(2,1)S(1)} %get-tuple-element.34), channel_id=1, source_target_pairs={{0,128},{16,144},{32,160},{48,176},{64,192},{80,208},{96,224},{112... | collective-permute-start | bytes 294920 | tf_op jit(solution)/shard_map/ppermute | solution.py:336
  30.3 5.6 %collective-permute-done.refs_0_ = bf16[96,512]{1,0:T(8,128)(2,1)S(1)} collective-permute-done((bf16[96,512]{1,0:T(8,128)(2,1)S(1)}, bf16[96,512]{1,0:T(8,128)(2,1)S(1)}, u32[]{:S(2)}, u32[]{:S(2)}) %collective-permute-start) | collective-permute-done | bytes 98336 | tf_op jit(solution)/shard_map/ppermute | solution.py:336
  36.0 5.7 %collective-permute-start.5 = (bf16[96,512]{1,0:T(8,128)(2,1)S(1)}, bf16[96,512]{1,0:T(8,128)(2,1)S(1)}, u32[]{:S(2)}, u32[]{:S(2)}) collective-permute-start(bf16[96,512]{1,0:T(8,128)(2,1)S(1)} %get-tuple-element.35), channel_id=1, source_target_pairs={{0,144},{16,128},{32,176},{48,160},{64,208},{80,192},{96,240},{112... | collective-permute-start | bytes 294920 | tf_op jit(solution)/shard_map/ppermute | solution.py:336
  41.7 0.0 collective-permute-start.6
  41.7 1.2 %collective-permute-done.2.refs_2_ = bf16[96,512]{1,0:T(8,128)(2,1)S(1)} collective-permute-done((bf16[96,512]{1,0:T(8,128)(2,1)S(1)}, bf16[96,512]{1,0:T(8,128)(2,1)S(1)}, u32[]{:S(2)}, u32[]{:S(2)}) %collective-permute-start.2) | collective-permute-done | bytes 98336 | tf_op jit(solution)/shard_map/ppermute | solution.py:336
  42.9 5.7 %collective-permute-start.7 = (bf16[96,512]{1,0:T(8,128)(2,1)S(1)}, bf16[96,512]{1,0:T(8,128)(2,1)S(1)}, u32[]{:S(2)}, u32[]{:S(2)}) collective-permute-start(bf16[96,512]{1,0:T(8,128)(2,1)S(1)} %get-tuple-element.37), channel_id=1, source_target_pairs={{0,176},{16,160},{32,208},{48,192},{64,240},{80,224},{96,16},{112,... | collective-permute-start | bytes 294920 | tf_op jit(solution)/shard_map/ppermute | solution.py:336
  48.6 0.0 collective-permute-done.4.refs_4_
  48.6 4.2 %collective-permute-start.9 = (bf16[96,512]{1,0:T(8,128)(2,1)S(1)}, bf16[96,512]{1,0:T(8,128)(2,1)S(1)}, u32[]{:S(2)}, u32[]{:S(2)}) collective-permute-start(bf16[96,512]{1,0:T(8,128)(2,1)S(1)} %get-tuple-element.39), channel_id=1, source_target_pairs={{0,192},{16,208},{32,224},{48,240},{64,0},{80,16},{96,32},{112,48}... | collective-permute-start | bytes 294920 | tf_op jit(solution)/shard_map/ppermute | solution.py:336
  52.8 1.7 %collective-permute-done.5.refs_5_ = bf16[96,512]{1,0:T(8,128)(2,1)S(1)} collective-permute-done((bf16[96,512]{1,0:T(8,128)(2,1)S(1)}, bf16[96,512]{1,0:T(8,128)(2,1)S(1)}, u32[]{:S(2)}, u32[]{:S(2)}) %collective-permute-start.5) | collective-permute-done | bytes 98336 | tf_op jit(solution)/shard_map/ppermute | solution.py:336
  54.5 0.4 collective-permute-start.10
  54.9 5.4 %collective-permute-done.6.refs_6_ = bf16[96,512]{1,0:T(8,128)(2,1)S(1)} collective-permute-done((bf16[96,512]{1,0:T(8,128)(2,1)S(1)}, bf16[96,512]{1,0:T(8,128)(2,1)S(1)}, u32[]{:S(2)}, u32[]{:S(2)}) %collective-permute-start.6) | collective-permute-done | bytes 98336 | tf_op jit(solution)/shard_map/ppermute | solution.py:336
  60.4 0.0 collective-permute-start.11
  60.4 3.0 %collective-permute-start.12 = (bf16[96,512]{1,0:T(8,128)(2,1)S(1)}, bf16[96,512]{1,0:T(8,128)(2,1)S(1)}, u32[]{:S(2)}, u32[]{:S(2)}) collective-permute-start(bf16[96,512]{1,0:T(8,128)(2,1)S(1)} %get-tuple-element.42), channel_id=1, source_target_pairs={{0,48},{16,32},{32,80},{48,64},{64,112},{80,96},{96,144},{112,128}... | collective-permute-start | bytes 294920 | tf_op jit(solution)/shard_map/ppermute | solution.py:336
  63.4 3.4 %collective-permute-start.13 = (bf16[96,512]{1,0:T(8,128)(2,1)S(1)}, bf16[96,512]{1,0:T(8,128)(2,1)S(1)}, u32[]{:S(2)}, u32[]{:S(2)}) collective-permute-start(bf16[96,512]{1,0:T(8,128)(2,1)S(1)} %get-tuple-element.43), channel_id=1, source_target_pairs={{0,240},{16,224},{32,16},{48,0},{64,48},{80,32},{96,80},{112,64},{... | collective-permute-start | bytes 294920 | tf_op jit(solution)/shard_map/ppermute | solution.py:336
  66.8 3.0 %shard_map.92 = (f32[48,384]{1,0:T(8,128)}, bf16[512,1024]{1,0:T(8,128)(2,1)S(1)}, bf16[512,1024]{1,0:T(8,128)(2,1)S(1)}, bf16[1024,384]{1,0:T(8,128)(2,1)S(1)}) custom-call(s32[1]{0:T(128)} %bitcast.1.me, bf16[768,768]{1,0:T(8,128)(2,1)S(1)} %get-tuple-element.28.pick, bf16[768,384]{1,0:T(8,128)(2,1)} %targets.1, bf16[512,1024]{1,0:T(8,128)(2,1)} %w_gate.3, ...), custom_call_target="tpu_custom_call" | custom-call | flops 10000000 | tf_op jit(solution)/shard_map/pallas_call | solution.py:348
  69.9 0.1 collective-permute-done.13.refs_13_
  70.1 0.4 copy-done.10
  70.5 0.0 copy-done.11
  70.5 0.0 copy-done.12
  70.6 0.1 copy-done.13
  70.6 0.0 copy-done.14
  70.7 15.9 %shard_map.94.earlier = f32[32,512]{1,0:T(8,128)} custom-call(bf16[96,512]{1,0:T(8,128)(2,1)} %copy-done, bf16[96,512]{1,0:T(8,128)(2,1)} %copy-done.1, bf16[96,512]{1,0:T(8,128)(2,1)} %copy-done.2, bf16[96,512]{1,0:T(8,128)(2,1)} %copy-done.3, bf16[96,512]{1,0:T(8,128)(2,1)} %copy-done.4, bf16[96,512]{1,0:T(8,128)(2,1)} %copy-done.5, ...), custom_call_target="tpu_custom_call" | custom-call | flops 10000000000 | tf_op jit(solution)/shard_map/pallas_call | solution.py:357
  86.6 8.7 %shard_map.95 = f32[16,16,128]{2,1,0:T(8,128)S(1)} custom-call(bf16[768,512]{1,0:T(8,128)(2,1)S(1)} %bitcast.3, f32[48,384]{1,0:T(8,128)} %get-tuple-element.29.refs_16_.target, bf16[512,1024]{1,0:T(8,128)(2,1)} %w_gate.3, bf16[512,1024]{1,0:T(8,128)(2,1)} %w_up.3, bf16[1024,384]{1,0:T(8,128)(2,1)} %lowering.3, f32[32,512]{1,0:T(8,128)} %shard_map.94.earlier), custom_call_target="tpu_custom_call" | custom-call | flops 5000000000 | tf_op jit(solution)/shard_map/pallas_call | solution.py:373
  95.3 12.8 %all_to_all.10.arrived = f32[16,16,128]{2,1,0:T(8,128)S(1)} all-to-all(f32[16,16,128]{2,1,0:T(8,128)S(1)} %shard_map.95), channel_id=1, replica_groups=mesh['member'=16,'space'=16] {'member'}, dimensions={0} | all-to-all | bytes 262144 | tf_op jit(solution)/shard_map/all_to_all | solution.py:376
  108.0 1.0 shard_map.96
  (37 shorter events, 0.1 us)
Async XLA Ops:
  3.8 82.8 %all-to-all-start = ((bf16[16,48,512]{2,1,0:T(8,128)(2,1)}), bf16[16,48,512]{2,1,0:T(8,128)(2,1)S(1)}, u32[]{:S(2)}, u32[]{:S(2)}) async-start(bf16[16,48,512]{2,1,0:T(8,128)(2,1)} %get-tuple-element.27), calls=%async_computation | async-start | bytes 1572864 | tf_op jit(solution)/shard_map/all_to_all | solution.py:346
  17.8 18.1 %collective-permute-start = (bf16[96,512]{1,0:T(8,128)(2,1)S(1)}, bf16[96,512]{1,0:T(8,128)(2,1)S(1)}, u32[]{:S(2)}, u32[]{:S(2)}) collective-permute-start(bf16[96,512]{1,0:T(8,128)(2,1)S(1)} %get-tuple-element.30), channel_id=1, source_target_pairs={{0,32},{16,48},{32,64},{48,80},{64,96},{80,112},{96,128},{112,144}... | collective-permute-start | bytes 294920 | tf_op jit(solution)/shard_map/ppermute | solution.py:336
  19.3 22.4 %collective-permute-start.1 = (bf16[96,512]{1,0:T(8,128)(2,1)S(1)}, bf16[96,512]{1,0:T(8,128)(2,1)S(1)}, u32[]{:S(2)}, u32[]{:S(2)}) collective-permute-start(bf16[96,512]{1,0:T(8,128)(2,1)S(1)} %get-tuple-element.31), channel_id=1, source_target_pairs={{0,224},{16,240},{32,0},{48,16},{64,32},{80,48},{96,64},{112,80},{... | collective-permute-start | bytes 294920 | tf_op jit(solution)/shard_map/ppermute | solution.py:336
  20.6 22.3 %collective-permute-start.2 = (bf16[96,512]{1,0:T(8,128)(2,1)S(1)}, bf16[96,512]{1,0:T(8,128)(2,1)S(1)}, u32[]{:S(2)}, u32[]{:S(2)}) collective-permute-start(bf16[96,512]{1,0:T(8,128)(2,1)S(1)} %get-tuple-element.32), channel_id=1, source_target_pairs={{0,96},{16,112},{32,128},{48,144},{64,160},{80,176},{96,192},{112,... | collective-permute-start | bytes 294920 | tf_op jit(solution)/shard_map/ppermute | solution.py:336
  23.5 25.1 %collective-permute-start.3 = (bf16[96,512]{1,0:T(8,128)(2,1)S(1)}, bf16[96,512]{1,0:T(8,128)(2,1)S(1)}, u32[]{:S(2)}, u32[]{:S(2)}) collective-permute-start(bf16[96,512]{1,0:T(8,128)(2,1)S(1)} %get-tuple-element.33), channel_id=1, source_target_pairs={{0,160},{16,176},{32,192},{48,208},{64,224},{80,240},{96,0},{112,1... | collective-permute-start | bytes 294920 | tf_op jit(solution)/shard_map/ppermute | solution.py:336
  25.1 23.5 %collective-permute-start.4 = (bf16[96,512]{1,0:T(8,128)(2,1)S(1)}, bf16[96,512]{1,0:T(8,128)(2,1)S(1)}, u32[]{:S(2)}, u32[]{:S(2)}) collective-permute-start(bf16[96,512]{1,0:T(8,128)(2,1)S(1)} %get-tuple-element.34), channel_id=1, source_target_pairs={{0,128},{16,144},{32,160},{48,176},{64,192},{80,208},{96,224},{112... | collective-permute-start | bytes 294920 | tf_op jit(solution)/shard_map/ppermute | solution.py:336
  36.0 34.1 %copy-start = (bf16[96,512]{1,0:T(8,128)(2,1)}, bf16[96,512]{1,0:T(8,128)(2,1)S(1)}, u32[]{:S(2)}) copy-start(bf16[96,512]{1,0:T(8,128)(2,1)S(1)} %collective-permute-done.refs_0_) | copy-start | bytes 294916
  36.0 18.5 %collective-permute-start.5 = (bf16[96,512]{1,0:T(8,128)(2,1)S(1)}, bf16[96,512]{1,0:T(8,128)(2,1)S(1)}, u32[]{:S(2)}, u32[]{:S(2)}) collective-permute-start(bf16[96,512]{1,0:T(8,128)(2,1)S(1)} %get-tuple-element.35), channel_id=1, source_target_pairs={{0,144},{16,128},{32,176},{48,160},{64,208},{80,192},{96,240},{112... | collective-permute-start | bytes 294920 | tf_op jit(solution)/shard_map/ppermute | solution.py:336
  41.7 28.3 %copy-start.1 = (bf16[96,512]{1,0:T(8,128)(2,1)}, bf16[96,512]{1,0:T(8,128)(2,1)S(1)}, u32[]{:S(2)}) copy-start(bf16[96,512]{1,0:T(8,128)(2,1)S(1)} %collective-permute-done.1.refs_1_) | copy-start | bytes 294916
  41.7 18.7 %collective-permute-start.6 = (bf16[96,512]{1,0:T(8,128)(2,1)S(1)}, bf16[96,512]{1,0:T(8,128)(2,1)S(1)}, u32[]{:S(2)}, u32[]{:S(2)}) collective-permute-start(bf16[96,512]{1,0:T(8,128)(2,1)S(1)} %get-tuple-element.36), channel_id=1, source_target_pairs={{0,112},{16,96},{32,144},{48,128},{64,176},{80,160},{96,208},{112,... | collective-permute-start | bytes 294920 | tf_op jit(solution)/shard_map/ppermute | solution.py:336
  42.9 27.1 %copy-start.2 = (bf16[96,512]{1,0:T(8,128)(2,1)}, bf16[96,512]{1,0:T(8,128)(2,1)S(1)}, u32[]{:S(2)}) copy-start(bf16[96,512]{1,0:T(8,128)(2,1)S(1)} %collective-permute-done.2.refs_2_) | copy-start | bytes 294916
  42.9 17.5 %collective-permute-start.7 = (bf16[96,512]{1,0:T(8,128)(2,1)S(1)}, bf16[96,512]{1,0:T(8,128)(2,1)S(1)}, u32[]{:S(2)}, u32[]{:S(2)}) collective-permute-start(bf16[96,512]{1,0:T(8,128)(2,1)S(1)} %get-tuple-element.37), channel_id=1, source_target_pairs={{0,176},{16,160},{32,208},{48,192},{64,240},{80,224},{96,16},{112,... | collective-permute-start | bytes 294920 | tf_op jit(solution)/shard_map/ppermute | solution.py:336
  48.6 21.4 %copy-start.3 = (bf16[96,512]{1,0:T(8,128)(2,1)}, bf16[96,512]{1,0:T(8,128)(2,1)S(1)}, u32[]{:S(2)}) copy-start(bf16[96,512]{1,0:T(8,128)(2,1)S(1)} %collective-permute-done.3.refs_3_) | copy-start | bytes 294916
  48.6 14.8 %collective-permute-start.8 = (bf16[96,512]{1,0:T(8,128)(2,1)S(1)}, bf16[96,512]{1,0:T(8,128)(2,1)S(1)}, u32[]{:S(2)}, u32[]{:S(2)}) collective-permute-start(bf16[96,512]{1,0:T(8,128)(2,1)S(1)} %get-tuple-element.38), channel_id=1, source_target_pairs={{0,64},{16,80},{32,96},{48,112},{64,128},{80,144},{96,160},{112,17... | collective-permute-start | bytes 294920 | tf_op jit(solution)/shard_map/ppermute | solution.py:336
  48.6 21.4 %copy-start.4 = (bf16[96,512]{1,0:T(8,128)(2,1)}, bf16[96,512]{1,0:T(8,128)(2,1)S(1)}, u32[]{:S(2)}) copy-start(bf16[96,512]{1,0:T(8,128)(2,1)S(1)} %collective-permute-done.4.refs_4_) | copy-start | bytes 294916
  48.6 18.2 %collective-permute-start.9 = (bf16[96,512]{1,0:T(8,128)(2,1)S(1)}, bf16[96,512]{1,0:T(8,128)(2,1)S(1)}, u32[]{:S(2)}, u32[]{:S(2)}) collective-permute-start(bf16[96,512]{1,0:T(8,128)(2,1)S(1)} %get-tuple-element.39), channel_id=1, source_target_pairs={{0,192},{16,208},{32,224},{48,240},{64,0},{80,16},{96,32},{112,48}... | collective-permute-start | bytes 294920 | tf_op jit(solution)/shard_map/ppermute | solution.py:336
  54.5 15.6 %copy-start.5 = (bf16[96,512]{1,0:T(8,128)(2,1)}, bf16[96,512]{1,0:T(8,128)(2,1)S(1)}, u32[]{:S(2)}) copy-start(bf16[96,512]{1,0:T(8,128)(2,1)S(1)} %collective-permute-done.5.refs_5_) | copy-start | bytes 294916
  54.5 15.4 %collective-permute-start.10 = (bf16[96,512]{1,0:T(8,128)(2,1)S(1)}, bf16[96,512]{1,0:T(8,128)(2,1)S(1)}, u32[]{:S(2)}, u32[]{:S(2)}) collective-permute-start(bf16[96,512]{1,0:T(8,128)(2,1)S(1)} %get-tuple-element.40), channel_id=1, source_target_pairs={{0,80},{16,64},{32,112},{48,96},{64,144},{80,128},{96,176},{112,16... | collective-permute-start | bytes 294920 | tf_op jit(solution)/shard_map/ppermute | solution.py:336
  60.4 9.7 %copy-start.6 = (bf16[96,512]{1,0:T(8,128)(2,1)}, bf16[96,512]{1,0:T(8,128)(2,1)S(1)}, u32[]{:S(2)}) copy-start(bf16[96,512]{1,0:T(8,128)(2,1)S(1)} %collective-permute-done.6.refs_6_) | copy-start | bytes 294916
  60.4 9.5 %collective-permute-start.11 = (bf16[96,512]{1,0:T(8,128)(2,1)S(1)}, bf16[96,512]{1,0:T(8,128)(2,1)S(1)}, u32[]{:S(2)}, u32[]{:S(2)}) collective-permute-start(bf16[96,512]{1,0:T(8,128)(2,1)S(1)} %get-tuple-element.41), channel_id=1, source_target_pairs={{0,208},{16,192},{32,240},{48,224},{64,16},{80,0},{96,48},{112,32}... | collective-permute-start | bytes 294920 | tf_op jit(solution)/shard_map/ppermute | solution.py:336
  60.4 9.7 %copy-start.7 = (bf16[96,512]{1,0:T(8,128)(2,1)}, bf16[96,512]{1,0:T(8,128)(2,1)S(1)}, u32[]{:S(2)}) copy-start(bf16[96,512]{1,0:T(8,128)(2,1)S(1)} %collective-permute-done.7.refs_7_) | copy-start | bytes 294916
  60.4 9.5 %collective-permute-start.12 = (bf16[96,512]{1,0:T(8,128)(2,1)S(1)}, bf16[96,512]{1,0:T(8,128)(2,1)S(1)}, u32[]{:S(2)}, u32[]{:S(2)}) collective-permute-start(bf16[96,512]{1,0:T(8,128)(2,1)S(1)} %get-tuple-element.42), channel_id=1, source_target_pairs={{0,48},{16,32},{32,80},{48,64},{64,112},{80,96},{96,144},{112,128}... | collective-permute-start | bytes 294920 | tf_op jit(solution)/shard_map/ppermute | solution.py:336
  63.4 6.7 %copy-start.8 = (bf16[96,512]{1,0:T(8,128)(2,1)}, bf16[96,512]{1,0:T(8,128)(2,1)S(1)}, u32[]{:S(2)}) copy-start(bf16[96,512]{1,0:T(8,128)(2,1)S(1)} %collective-permute-done.8.refs_8_) | copy-start | bytes 294916
  63.4 6.6 %collective-permute-start.13 = (bf16[96,512]{1,0:T(8,128)(2,1)S(1)}, bf16[96,512]{1,0:T(8,128)(2,1)S(1)}, u32[]{:S(2)}, u32[]{:S(2)}) collective-permute-start(bf16[96,512]{1,0:T(8,128)(2,1)S(1)} %get-tuple-element.43), channel_id=1, source_target_pairs={{0,240},{16,224},{32,16},{48,0},{64,48},{80,32},{96,80},{112,64},{... | collective-permute-start | bytes 294920 | tf_op jit(solution)/shard_map/ppermute | solution.py:336
  66.8 3.3 %copy-start.9 = (bf16[96,512]{1,0:T(8,128)(2,1)}, bf16[96,512]{1,0:T(8,128)(2,1)S(1)}, u32[]{:S(2)}) copy-start(bf16[96,512]{1,0:T(8,128)(2,1)S(1)} %collective-permute-done.9.refs_9_) | copy-start | bytes 294916
  66.8 3.2 %collective-permute-start.14 = (bf16[96,512]{1,0:T(8,128)(2,1)S(1)}, bf16[96,512]{1,0:T(8,128)(2,1)S(1)}, u32[]{:S(2)}, u32[]{:S(2)}) collective-permute-start(bf16[96,512]{1,0:T(8,128)(2,1)S(1)} %get-tuple-element.44), channel_id=1, source_target_pairs={{0,16},{16,0},{32,48},{48,32},{64,80},{80,64},{96,112},{112,96},{1... | collective-permute-start | bytes 294920 | tf_op jit(solution)/shard_map/ppermute | solution.py:336
  69.8 0.6 copy-start.10
  69.8 0.7 copy-start.11
  69.9 0.7 copy-start.12
  70.0 0.6 copy-start.13
  70.0 0.7 copy-start.14
